TPU v7x, 8 devices: a whole 2x2x1 slice. The times are simulated.
8 devices in a mesh: dp: 1 (over z), ep: 8 (over y, x, core).
Axes of the slice: x: 2, y: 2, z: 1, core: 2. Of those that a mesh axis runs over, the one named last changes fastest.
Arguments:
- tokens: bfloat16 [8, 1024, 1024], P(('dp', 'ep'))
- w_gate: bfloat16 [1024, 32], replicated
- expert_ids: int32 [8, 1024, 2], P(('dp', 'ep'))
- keep_second: int32 [8, 1024], P(('dp', 'ep'))
- w_in: bfloat16 [32, 1024, 2816], P('ep')
- w_out: bfloat16 [32, 2816, 1024], P('ep')
Outputs:
- output: bfloat16 [8, 1024, 1024], P(('dp', 'ep'))
All inputs are finite; a program needn't handle non-finite values.
Results may differ from a plain program's by a relative error of at most 0.001.
Values are sent between devices in bfloat16 or wider.
A program may use at most 1 GiB of HBM per device.

v0:
```python
import jax
import jax.numpy as jnp
from jax import lax
from jax.sharding import PartitionSpec as P


def build_routing(tokens, w_gate, expert_ids, keep_second, capacity):
    expert_count = w_gate.shape[1]
    logits = jnp.einsum("gsm,me->gse", tokens, w_gate, preferred_element_type=jnp.float32)
    gate_probs = jax.nn.softmax(logits, axis=-1)
    first_hot = jax.nn.one_hot(expert_ids[:, :, 0], expert_count, dtype=jnp.int32)
    second_hot = jax.nn.one_hot(expert_ids[:, :, 1], expert_count, dtype=jnp.int32) * keep_second[:, :, None]
    gate_first = jnp.sum(gate_probs * first_hot, axis=-1)
    gate_second = jnp.sum(gate_probs * second_hot, axis=-1)
    gate_total = gate_first + gate_second
    pos_first = jnp.sum((jnp.cumsum(first_hot, axis=1) - first_hot) * first_hot, axis=-1)
    second_base = jnp.cumsum(second_hot, axis=1) - second_hot + jnp.sum(first_hot, axis=1, keepdims=True)
    pos_second = jnp.sum(second_base * second_hot, axis=-1)
    slot_first = first_hot.astype(jnp.bfloat16)[:, :, :, None] * jax.nn.one_hot(pos_first, capacity, dtype=jnp.bfloat16)[:, :, None, :]
    slot_second = second_hot.astype(jnp.bfloat16)[:, :, :, None] * jax.nn.one_hot(pos_second, capacity, dtype=jnp.bfloat16)[:, :, None, :]
    dispatch = slot_first + slot_second
    weight_first = (gate_first / gate_total).astype(jnp.bfloat16)[:, :, None, None]
    weight_second = (gate_second / gate_total).astype(jnp.bfloat16)[:, :, None, None]
    combine = weight_first * slot_first + weight_second * slot_second
    return dispatch, combine


def solution(mesh):
    group_count = mesh.shape["ep"]

    def local_layer(tokens, w_gate, expert_ids, keep_second, w_in, w_out):
        token_count = tokens.shape[1]
        model_dim = tokens.shape[2]
        expert_count = w_gate.shape[1]
        local_experts = w_in.shape[0]
        capacity = 2 * token_count // expert_count
        dispatch, combine = build_routing(tokens, w_gate, expert_ids, keep_second, capacity)
        send_rows = jnp.einsum("gsec,gsm->ecm", dispatch, tokens, preferred_element_type=jnp.float32).astype(jnp.bfloat16)
        send_rows = send_rows.reshape(group_count, local_experts, capacity, model_dim)
        recv_rows = lax.all_to_all(send_rows, "ep", 0, 0, tiled=True)
        hidden = jax.nn.relu(jnp.einsum("gecm,emh->egch", recv_rows, w_in, preferred_element_type=jnp.float32)).astype(jnp.bfloat16)
        back_rows = jnp.einsum("egch,ehm->gecm", hidden, w_out, preferred_element_type=jnp.float32).astype(jnp.bfloat16)
        back_rows = lax.all_to_all(back_rows, "ep", 0, 0, tiled=True)
        back_rows = back_rows.reshape(expert_count, capacity, model_dim)
        mixed_rows = jnp.einsum("gsec,ecm->gsm", combine, back_rows, preferred_element_type=jnp.float32)
        return mixed_rows.astype(jnp.bfloat16)

    group_spec = P(("dp", "ep"))
    return jax.shard_map(local_layer, mesh=mesh, in_specs=(group_spec, P(), group_spec, group_spec, P("ep"), P("ep")), out_specs=group_spec, check_vma=False)
```

profile of v0, /device:TPU:0, one launch (start us, length us, event | category | flops | bytes accessed | tf_op | source)
XLA Modules:
  0.0 191.4 jit_solution(6204342103718122132)
XLA Ops:
  0.0 0.0 copy-start
  0.0 0.9 fusion.46
  0.9 0.7 select_convert_fusion
  1.6 0.7 select_bitcast_fusion
  2.3 9.0 %reduce-window.16 = s32[1,32,8,128]{3,2,1,0:T(8,128)S(1)} reduce-window(s32[1,32,8,128]{3,2,1,0:T(8,128)S(1)} %bitcast.62, s32[]{:T(128)} %constant.14.clone.1), window={size=1x1x1x128 pad=0_0x0_0x0_0x127_0}, to_apply=%region_7.8 | reduce-window | flops 4161536 | bytes 262148 | tf_op jit(solution)/shard_map/reduce-window.2
  11.3 0.1 slice.26
  11.6 9.0 %reduce-window.14 = s32[1,32,8,128]{3,2,1,0:T(8,128)S(1)} reduce-window(s32[1,32,8,128]{3,2,1,0:T(8,128)S(1)} %bitcast.63, s32[]{:T(128)} %constant.14.clone.1), window={size=1x1x1x128 pad=0_0x0_0x0_0x127_0}, to_apply=%region_4.5 | reduce-window | flops 4161536 | bytes 262148 | tf_op jit(solution)/shard_map/reduce-window
  20.6 0.1 slice.24
  20.7 0.1 copy.20
  20.9 0.1 copy.21
  20.9 0.1 broadcast.221
  21.1 0.1 copy.18
  21.2 0.1 copy.19
  21.3 0.1 broadcast.219
  21.5 0.1 fusion.34
  21.6 0.8 fusion.40
  22.4 0.1 fusion.31
  22.4 0.0 copy-done
  22.5 4.7 %fusion.10 = bf16[32,64,1024]{2,1,0:T(8,128)(2,1)S(1)} fusion(bf16[1,1024,1024]{2,1,0:T(8,128)(2,1)S(1)} %copy-done, bf16[1024,64]{0,1:T(8,128)(2,1)S(1)} %get-tuple-element.16, bf16[1024,32]{0,1:T(8,128)(2,1)S(1)} %select_convert_fusion, bf16[1024,64]{0,1:T(8,128)(2,1)S(1)} %get-tuple-element.15, bf16[1024,32]{0,1:T(8,128)(2,1)S(1)} %convert_convert_fusion), kind=kOutput, calls=%fused_computation.15 | convolution fusion | flops 4303355904 | bytes 6684672 | tf_op jit(solution)/shard_map/gsec,gsm->ecm/dot_general | solution.py:38
  27.2 53.1 %all_to_all.10 = bf16[8,4,64,1024]{3,2,1,0:T(8,128)(2,1)} all-to-all(bf16[8,4,64,1024]{3,2,1,0:T(8,128)(2,1)S(1)} %bitcast.61), channel_id=1, replica_groups=mesh['dp'=1,'ep'=8] {'ep'}, dimensions={0} | all-to-all | bytes 8388608 | tf_op jit(solution)/shard_map/all_to_all | solution.py:40
  80.3 23.0 %fusion.2 = bf16[4,8,64,2816]{3,2,1,0:T(8,128)(2,1)} fusion(bf16[4,1024,2816]{2,1,0:T(8,128)(2,1)} %param.10, bf16[8,4,64,1024]{3,2,1,0:T(8,128)(2,1)} %all_to_all.10), kind=kOutput, calls=%fused_computation.2 | convolution fusion | flops 11811160064 | bytes 38797312 | tf_op jit(solution)/shard_map/gecm,emh->egch/dot_general | solution.py:41
  103.3 22.8 %convert_bitcast_fusion = bf16[8,4,64,1024]{3,2,0,1:T(8,128)(2,1)} fusion(bf16[4,2816,1024]{2,1,0:T(8,128)(2,1)} %param.11, bf16[4,8,64,2816]{3,2,1,0:T(8,128)(2,1)} %fusion.2), kind=kOutput, calls=%fused_computation.14 | convolution fusion | flops 11830558720 | bytes 38797312 | tf_op jit(solution)/shard_map/egch,ehm->gecm/dot_general | solution.py:42
  126.1 4.8 %copy.23 = bf16[8,4,64,1024]{3,2,1,0:T(8,128)(2,1)} copy(bf16[8,4,64,1024]{3,2,0,1:T(8,128)(2,1)} %convert_bitcast_fusion) | data formatting | bytes 8388608 | tf_op jit(solution)/shard_map/convert_element_type | solution.py:42
  131.0 0.0 copy-start.2
  131.0 0.0 copy-start.1
  131.0 3.6 %all-to-all-start.1 = ((bf16[8,4,64,1024]{3,2,1,0:T(8,128)(2,1)}), bf16[8,4,64,1024]{3,2,1,0:T(8,128)(2,1)}, u32[]{:S(2)}, u32[]{:S(2)}) async-start(bf16[8,4,64,1024]{3,2,1,0:T(8,128)(2,1)} %copy.23), calls=%async_computation.1 | async-start | bytes 8388608 | tf_op jit(solution)/shard_map/all_to_all | solution.py:43
  134.6 0.0 copy-done.2
  134.6 0.7 fusion.47
  135.4 0.0 copy-done.1
  135.4 0.1 fusion.38
  135.5 47.9 %all-to-all-done.1 = bf16[8,4,64,1024]{3,2,1,0:T(8,128)(2,1)} async-done(((bf16[8,4,64,1024]{3,2,1,0:T(8,128)(2,1)}), bf16[8,4,64,1024]{3,2,1,0:T(8,128)(2,1)}, u32[]{:S(2)}, u32[]{:S(2)}) %all-to-all-start.1) | async-done | bytes 4194336 | tf_op jit(solution)/shard_map/all_to_all | solution.py:43
  183.4 8.0 %fusion.28 = bf16[1,1024,1024]{2,1,0:T(8,128)(2,1)} fusion(bf16[32,64,1024]{2,1,0:T(8,128)(2,1)} %bitcast.19, bf16[1024,64]{0,1:T(8,128)(2,1)S(1)} %get-tuple-element.16, bf16[1024,32]{0,1:T(8,128)(2,1)S(1)} %select_convert_fusion, bf16[1024]{0:T(1024)(128)(2,1)S(1)} %get-tuple-element.10, bf16[1024,64]{0,1:T(8,128)(2,1)S(1)} %get-tuple-element.15, ...), kind=kOutput, calls=%fused_computation.29 | convolution fusion | flops 4306501632 | bytes 6688768 | tf_op jit(solution)/shard_map/gsec,ecm->gsm/dot_general | solution.py:45
  (14 shorter events, 0.3 us)
Async XLA Ops:
  0.0 22.4 %copy-start = (bf16[1,1024,1024]{2,1,0:T(8,128)(2,1)S(1)}, bf16[1,1024,1024]{2,1,0:T(8,128)(2,1)}, u32[]{:S(2)}) copy-start(bf16[1,1024,1024]{2,1,0:T(8,128)(2,1)} %param.6) | copy-start | bytes 6291460
  131.0 3.6 %copy-start.2 = (bf16[1024,32]{0,1:T(8,128)(2,1)S(1)}, bf16[1024,32]{0,1:T(8,128)(2,1)}, u32[]{:S(2)}) copy-start(bf16[1024,32]{0,1:T(8,128)(2,1)} %param.7) | copy-start | bytes 196612
  131.0 4.4 %copy-start.1 = (s32[1,1024]{1,0:T(1,128)S(1)}, s32[1,1024]{1,0:T(1,128)}, u32[]{:S(2)}) copy-start(s32[1,1024]{1,0:T(1,128)} %param.9) | copy-start | bytes 12292
  131.0 52.4 %all-to-all-start.1 = ((bf16[8,4,64,1024]{3,2,1,0:T(8,128)(2,1)}), bf16[8,4,64,1024]{3,2,1,0:T(8,128)(2,1)}, u32[]{:S(2)}, u32[]{:S(2)}) async-start(bf16[8,4,64,1024]{3,2,1,0:T(8,128)(2,1)} %copy.23), calls=%async_computation.1 | async-start | bytes 8388608 | tf_op jit(solution)/shard_map/all_to_all | solution.py:43
where the time goes:
time: 192 us; the launch traced here: 191 us
  matrix products  59.3 us (31%)
  blocking collectives  53.1 us (28%)
  waiting for transfers between devices  47.9 us (25%)
  other arithmetic  20.6 us (11%)
  local copies, waits for them, and re-layouts  6.66 us (3%)
  starting transfers between devices  3.63 us (2%)
    all_to_all x1, blocking collectives, local_layer(): recv_rows = lax.all_to_all(send_rows, 'ep', 0, 0, tiled=True)  53.1 us
    all_to_all x1, waiting for transfers between devices, local_layer(): back_rows = lax.all_to_all(back_rows, 'ep', 0, 0, tiled=True)  47.9 us
    dot_general x1, matrix products, local_layer(): jnp.einsum('gecm,emh->egch', recv_rows, w_in, preferred_element_type=jnp....  23 us
    dot_general x1, matrix products, local_layer(): jnp.einsum('egch,ehm->gecm', hidden, w_out, preferred_element_type=jnp.fl...  22.8 us
    another operation x4, other arithmetic  18.1 us
    dot_general x1, matrix products, local_layer(): jnp.einsum('gsec,ecm->gsm', combine, back_rows, preferred_element_type=jn...  8.02 us
    convert_element_type x1, local copies, waits for them, and re-layouts, local_layer(): jnp.einsum('egch,ehm->gecm', hidden, w_out, preferred_element_type=jnp.fl...  4.83 us
    dot_general x1, matrix products, local_layer(): jnp.einsum('gsec,gsm->ecm', dispatch, tokens, preferred_element_type=jnp....  4.71 us
  transfers between devices with their start and end apart: 1, of which 1 were waited for; matrix products, arithmetic and copies ran while one was open for 0% of the time, Pallas kernels for 0%

commit v1 on v0

v1 whole, which is shorter than its diff:
```python
import functools

import jax
import jax.numpy as jnp
from jax import lax
from jax.experimental import pallas as pl
from jax.experimental.pallas import tpu as pltpu
from jax.sharding import PartitionSpec as P

MESH = pl.DeviceIdType.MESH
SEND_ORDER = (6, 7, 2, 4, 3, 5, 1)


def peer_of(me, k):
    core, x, y = me % 2, (me // 2) % 2, me // 4
    core_bit, x_bit, y_bit = k % 2, (k // 2) % 2, k // 4
    core = 1 - core if core_bit else core
    x = 1 - x if x_bit else x
    y = 1 - y if y_bit else y
    return (y * 2 + x) * 2 + core


def layer_kernel(
    cap, tok_hbm, wg_hbm, ids_hbm, keep_hbm, win_hbm, wout_hbm, out_hbm,
    tok, wg, ids, keep, keys, gates, cols, dmat, xs, xr, ys, yr, hid, wi, wo, cw, acc, obuf,
    in_sem, wi_sem, wo_sem, xs_sem, xr_sem, ys_sem, yr_sem, out_sem,
):
    me = lax.axis_index("ep")
    experts_here = win_hbm.shape[0]
    tokens, dim = tok.shape
    experts = wg.shape[0]
    hidden = hid.shape[1]
    groups = experts // experts_here
    rows = groups * cap
    f32, bf16 = jnp.float32, jnp.bfloat16

    barrier = pltpu.get_barrier_semaphore()
    for k in range(1, 8):
        pl.semaphore_signal(barrier, inc=1, device_id={"ep": peer_of(me, k)}, device_id_type=MESH)

    small = [
        pltpu.make_async_copy(ids_hbm, ids, in_sem.at[0]),
        pltpu.make_async_copy(keep_hbm, keep, in_sem.at[1]),
        pltpu.make_async_copy(tok_hbm, tok, in_sem.at[2]),
        pltpu.make_async_copy(wg_hbm, wg, in_sem.at[3]),
    ]
    for copy in small:
        copy.start()

    def wi_copy(e):
        return pltpu.make_async_copy(win_hbm.at[e], wi.at[e % 2], wi_sem.at[e % 2])

    def wo_copy(e):
        return pltpu.make_async_copy(wout_hbm.at[e], wo.at[e % 2], wo_sem.at[e % 2])

    for e in range(2):
        wi_copy(e).start()
        wo_copy(e).start()

    small[0].wait()
    small[1].wait()
    expert_row = lax.broadcasted_iota(jnp.int32, (experts, tokens), 0)
    id1, id2, kept2 = ids[0:1, :], ids[1:2, :], keep[0:1, :]
    hot1 = (expert_row == id1).astype(f32)
    hot2 = ((expert_row == id2) & (kept2 > 0)).astype(f32)
    hot = jnp.concatenate([hot1, hot2], axis=0).astype(bf16)
    blk = 256
    r_io = lax.broadcasted_iota(jnp.int32, (blk, blk), 0)
    c_io = lax.broadcasted_iota(jnp.int32, (blk, blk), 1)
    before = jnp.where(r_io < c_io, 1.0, 0.0).astype(bf16)
    ones = jnp.ones((blk, blk), bf16)
    seen = jnp.zeros((2 * experts, blk), f32)
    earlier = []
    for b in range(tokens // blk):
        part = hot[:, b * blk:(b + 1) * blk]
        earlier.append(jnp.dot(part, before, preferred_element_type=f32) + seen)
        seen = seen + jnp.dot(part, ones, preferred_element_type=f32)
    first_total = seen[:experts, :]
    pos1 = jnp.concatenate([jnp.sum(p[:experts] * hot1[:, b * blk:(b + 1) * blk], axis=0, keepdims=True) for b, p in enumerate(earlier)], axis=1)
    pos2 = jnp.concatenate([jnp.sum((p[experts:] + first_total) * hot2[:, b * blk:(b + 1) * blk], axis=0, keepdims=True) for b, p in enumerate(earlier)], axis=1)
    pos1, pos2 = pos1.astype(jnp.int32), pos2.astype(jnp.int32)
    key1 = jnp.where(pos1 < cap, id1 * cap + pos1, -1)
    key2 = jnp.where((pos2 < cap) & (kept2 > 0), id2 * cap + pos2, -1)
    keys[0:1, :] = key1
    keys[1:2, :] = key2

    def x_send(e, k):
        peer = peer_of(me, k)
        return pltpu.make_async_remote_copy(
            src_ref=xs.at[e, pl.ds(pl.multiple_of(peer * cap, cap), cap)],
            dst_ref=xr.at[e, pl.ds(pl.multiple_of(me * cap, cap), cap)],
            send_sem=xs_sem.at[e, k], recv_sem=xr_sem.at[e, k],
            device_id={"ep": peer}, device_id_type=MESH,
        )

    def y_send(e, k):
        peer = peer_of(me, k)
        return pltpu.make_async_remote_copy(
            src_ref=ys.at[e, pl.ds(pl.multiple_of(peer * cap, cap), cap)],
            dst_ref=yr.at[e, pl.ds(pl.multiple_of(me * cap, cap), cap)],
            send_sem=ys_sem.at[e, k], recv_sem=yr_sem.at[e, k],
            device_id={"ep": peer}, device_id_type=MESH,
        )

    mine = pl.ds(pl.multiple_of(me * cap, cap), cap)

    def dispatch(e):
        row = lax.broadcasted_iota(jnp.int32, (rows, tokens), 0)
        slot = (row // cap) * (experts_here * cap) + e * cap + row % cap
        hit = (slot == keys[0:1, :]) | (slot == keys[1:2, :])
        dmat[...] = jnp.where(hit, 1.0, 0.0).astype(bf16)

        def columns(n, _):
            at = pl.ds(pl.multiple_of(n * blk, blk), blk)
            xs[e, :, at] = jnp.dot(dmat[...], tok[:, at], preferred_element_type=f32).astype(bf16)
            return 0

        lax.fori_loop(0, dim // blk, columns, 0)
        xr[e, mine] = xs[e, mine]

    small[2].wait()
    dispatch(0)
    pl.semaphore_wait(barrier, 7)
    for k in SEND_ORDER:
        x_send(0, k).start()

    def dispatch_rest(e, _):
        dispatch(e)
        for k in SEND_ORDER:
            x_send(e, k).start()
        return 0

    lax.fori_loop(1, experts_here, dispatch_rest, 0)

    small[3].wait()
    logits = lax.dot_general(wg[...], tok[...], (((1,), (1,)), ((), ())), preferred_element_type=f32)
    top = jnp.max(logits, axis=0, keepdims=True)
    expd = jnp.exp(logits - top)
    probs = expd / jnp.sum(expd, axis=0, keepdims=True)
    gate1 = jnp.sum(jnp.where(expert_row == ids[0:1, :], probs, 0.0), axis=0, keepdims=True)
    gate2 = jnp.sum(jnp.where((expert_row == ids[1:2, :]) & (keep[0:1, :] > 0), probs, 0.0), axis=0, keepdims=True)
    total = gate1 + gate2
    gates[0:1, :] = keys[0:1, :].astype(f32)
    gates[1:2, :] = keys[1:2, :].astype(f32)
    gates[2:3, :] = gate1 / total
    gates[3:4, :] = gate2 / total
    gates[4:, :] = jnp.zeros((gates.shape[0] - 4, tokens), f32)
    cols[...] = gates[...].T

    def weights(e, _):
        def block(t, _):
            at = pl.ds(pl.multiple_of(t * blk, blk), blk)
            lane = lax.broadcasted_iota(jnp.int32, (blk, rows), 1)
            slot = ((lane // cap) * (experts_here * cap) + e * cap + lane % cap).astype(f32)
            part = cols[at, :]
            cw[e, at, :] = (
                jnp.where(slot == part[:, 0:1], part[:, 2:3], 0.0) + jnp.where(slot == part[:, 1:2], part[:, 3:4], 0.0)
            ).astype(bf16)
            return 0

        return lax.fori_loop(0, tokens // blk, block, 0)

    lax.fori_loop(0, experts_here, weights, 0)

    def expert(e, _):
        s = e % 2
        for k in SEND_ORDER:
            x_send(e, k).wait_recv()
        wi_copy(e).wait()

        def up(j, _):
            at = pl.ds(pl.multiple_of(j * blk, blk), blk)
            pre = jnp.dot(xr[e], wi[s, :, at], preferred_element_type=f32)
            hid[:, at] = jnp.maximum(pre, 0.0).astype(bf16)
            return 0

        lax.fori_loop(0, hidden // blk, up, 0)

        @pl.when(e + 2 < experts_here)
        def _():
            wi_copy(e + 2).start()

        wo_copy(e).wait()

        def down(n, _):
            at = pl.ds(pl.multiple_of(n * blk, blk), blk)
            ys[e, :, at] = jnp.dot(hid[...], wo[s, :, at], preferred_element_type=f32).astype(bf16)
            return 0

        lax.fori_loop(0, dim // blk, down, 0)

        @pl.when(e + 2 < experts_here)
        def _():
            wo_copy(e + 2).start()

        for k in SEND_ORDER:
            y_send(e, k).start()
        yr[e, mine] = ys[e, mine]
        return 0

    lax.fori_loop(0, experts_here, expert, 0)

    def back(e):
        for k in SEND_ORDER:
            y_send(e, k).wait_recv()

    back(0)

    def first_columns(n, _):
        at = pl.ds(pl.multiple_of(n * blk, blk), blk)
        acc[:, at] = jnp.dot(cw[0], yr[0, :, at], preferred_element_type=f32)
        return 0

    lax.fori_loop(0, dim // blk, first_columns, 0)

    def combine(e, _):
        back(e)

        def columns(n, _):
            at = pl.ds(pl.multiple_of(n * blk, blk), blk)
            acc[:, at] += jnp.dot(cw[e], yr[e, :, at], preferred_element_type=f32)
            return 0

        return lax.fori_loop(0, dim // blk, columns, 0)

    lax.fori_loop(1, experts_here - 1, combine, 0)
    last = experts_here - 1
    back(last)

    def out_copy(t):
        at = pl.ds(pl.multiple_of(t * blk, blk), blk)
        return pltpu.make_async_copy(obuf.at[at], out_hbm.at[at], out_sem.at[t])

    def finish(t, _):
        at = pl.ds(pl.multiple_of(t * blk, blk), blk)
        obuf[at, :] = (acc[at, :] + jnp.dot(cw[last, at, :], yr[last], preferred_element_type=f32)).astype(bf16)
        out_copy(t).start()
        return 0

    lax.fori_loop(0, tokens // blk, finish, 0)

    def drain(e, _):
        for k in SEND_ORDER:
            x_send(e, k).wait_send()
            y_send(e, k).wait_send()
        return 0

    lax.fori_loop(0, experts_here, drain, 0)
    for t in range(tokens // blk):
        out_copy(t).wait()


def solution(mesh):
    def local_layer(tokens, w_gate, expert_ids, keep_second, w_in, w_out):
        _, token_count, dim = tokens.shape
        experts = w_gate.shape[1]
        here, _, hidden = w_in.shape
        cap = 2 * token_count // experts
        groups = experts // here
        rows = groups * cap
        f32, bf16 = jnp.float32, jnp.bfloat16
        vmem, dma = pltpu.VMEM, pltpu.SemaphoreType.DMA
        out = pl.pallas_call(
            functools.partial(layer_kernel, cap),
            out_shape=jax.ShapeDtypeStruct((token_count, dim), bf16),
            in_specs=[pl.BlockSpec(memory_space=pl.ANY)] * 6,
            out_specs=pl.BlockSpec(memory_space=pl.ANY),
            scratch_shapes=[
                vmem((token_count, dim), bf16),
                vmem((experts, dim), bf16),
                vmem((2, token_count), jnp.int32),
                vmem((1, token_count), jnp.int32),
                vmem((8, token_count), jnp.int32),
                vmem((128, token_count), f32),
                vmem((token_count, 128), f32),
                vmem((rows, token_count), bf16),
                vmem((here, rows, dim), bf16),
                vmem((here, rows, dim), bf16),
                vmem((here, rows, dim), bf16),
                vmem((here, rows, dim), bf16),
                vmem((rows, hidden), bf16),
                vmem((2, dim, hidden), bf16),
                vmem((2, hidden, dim), bf16),
                vmem((here, token_count, rows), bf16),
                vmem((token_count, dim), f32),
                vmem((token_count, dim), bf16),
                dma((4,)), dma((2,)), dma((2,)),
                dma((here, groups)), dma((here, groups)), dma((here, groups)), dma((here, groups)),
                dma((4,)),
            ],
            compiler_params=pltpu.CompilerParams(collective_id=0, has_side_effects=True, vmem_limit_bytes=67043328),
            name="moe_layer",
        )(tokens[0], w_gate.T, expert_ids[0].T, keep_second, w_in, w_out)
        return out[None]

    group_spec = P(("dp", "ep"))
    return jax.shard_map(local_layer, mesh=mesh, in_specs=(group_spec, P(), group_spec, group_spec, P("ep"), P("ep")), out_specs=group_spec, check_vma=False)
```

time: 192 us -> 104 us (0.54)
  Pallas kernels: 0 us -> 101 us
  matrix products: 59.3 us -> 0 us
  blocking collectives: 53.1 us -> 0 us
  waiting for transfers between devices: 47.9 us -> 0 us
  other arithmetic: 20.6 us -> 0 us
  starting transfers between devices: 3.63 us -> 0 us
  local copies, waits for them, and re-layouts: 6.66 us -> 3.08 us
    pallas_call x0 -> x1, Pallas kernels: none -> 101 us  [local_layer(): pl.pallas_call(functools.partial(layer_kernel, cap), out_shape=jax.ShapeD...]
    dot_general x5 -> x0, matrix products: 59.3 us -> none  [the longest x1 23 us: local_layer(): jnp.einsum('gecm,emh->egch', recv_rows, w_in, preferred_element_type=jnp....]
    all_to_all x1 -> x0, blocking collectives: 53.1 us -> none  [local_layer(): recv_rows = lax.all_to_all(send_rows, 'ep', 0, 0, tiled=True)]
    all_to_all x1 -> x0, waiting for transfers between devices: 47.9 us -> none  [local_layer(): back_rows = lax.all_to_all(back_rows, 'ep', 0, 0, tiled=True)]
    another operation x4 -> x0, other arithmetic: 18.1 us -> none
    convert_element_type x1 -> x0, local copies, waits for them, and re-layouts: 4.83 us -> none  [local_layer(): jnp.einsum('egch,ehm->gecm', hidden, w_out, preferred_element_type=jnp.fl...]
    all_to_all x1 -> x0, starting transfers between devices: 3.63 us -> none  [local_layer(): back_rows = lax.all_to_all(back_rows, 'ep', 0, 0, tiled=True)]
    unnamed x8 -> x1, local copies, waits for them, and re-layouts: 0.06 us -> 3.08 us
  transfers between devices with their start and end apart: 1 -> 0, of which waited for: 1 -> 0; matrix products, arithmetic and copies ran while one was open for 0% -> 0% of each run, Pallas kernels for 0% -> 0%
where the time goes in v1:
time: 104 us
  Pallas kernels  101 us (97%)
  local copies, waits for them, and re-layouts  3.08 us (3%)
    pallas_call x1, Pallas kernels, local_layer(): pl.pallas_call(functools.partial(layer_kernel, cap), out_shape=jax.ShapeD...  101 us
    unnamed x1, local copies, waits for them, and re-layouts  3.08 us

profile of v1, /device:TPU:0, one launch (start us, length us, event | category | flops | bytes accessed | tf_op | source)
XLA Modules:
  0.0 103.8 jit_solution(5457588089488462990)
XLA Ops:
  0.0 100.7 %moe_layer.1 = bf16[1024,1024]{1,0:T(8,128)(2,1)} custom-call(bf16[1024,1024]{1,0:T(8,128)(2,1)} %bitcast.7, bf16[32,1024]{1,0:T(8,128)(2,1)} %bitcast.8, s32[2,1024]{1,0:T(2,128)} %bitcast.9, s32[1,1024]{1,0:T(1,128)} %keep_hbm.1, bf16[4,1024,2816]{2,1,0:T(8,128)(2,1)} %win_hbm.1, bf16[4,2816,1024]{2,1,0:T(8,128)(2,1)} %wout_hbm.1), custom_call_target="tpu_custom_call" | custom-call | tf_op jit(solution)/shard_map/moe_layer/pallas_call | solution.py:263
  100.8 3.1 %copy.8 = bf16[1,1024,1024]{2,1,0:T(8,128)(2,1)} copy(bf16[1,1024,1024]{2,1,0:T(8,128)(2,1)} %bitcast.6) | data formatting | bytes 4194304

commit v2 on v1

--- a/solution.py
+++ b/solution.py
@@ -21,9 +21,9 @@
 
 
 def layer_kernel(
-    cap, tok_hbm, wg_hbm, ids_hbm, keep_hbm, win_hbm, wout_hbm, out_hbm,
-    tok, wg, ids, keep, keys, gates, cols, dmat, xs, xr, ys, yr, hid, wi, wo, cw, acc, obuf,
-    in_sem, wi_sem, wo_sem, xs_sem, xr_sem, ys_sem, yr_sem, out_sem,
+    cap, tok_hbm, wg_hbm, ids_hbm, keep_hbm, win_hbm, wout_hbm, obuf,
+    tok, wg, ids, keep, keys, gates, cols, dmat, xs, xr, ys, yr, hid, wi, wo, cw, acc,
+    in_sem, wi_sem, wo_sem, xs_sem, xr_sem, ys_sem, yr_sem,
 ):
     me = lax.axis_index("ep")
     experts_here = win_hbm.shape[0]
@@ -227,14 +227,9 @@
     last = experts_here - 1
     back(last)
 
-    def out_copy(t):
-        at = pl.ds(pl.multiple_of(t * blk, blk), blk)
-        return pltpu.make_async_copy(obuf.at[at], out_hbm.at[at], out_sem.at[t])
-
     def finish(t, _):
         at = pl.ds(pl.multiple_of(t * blk, blk), blk)
         obuf[at, :] = (acc[at, :] + jnp.dot(cw[last, at, :], yr[last], preferred_element_type=f32)).astype(bf16)
-        out_copy(t).start()
         return 0
 
     lax.fori_loop(0, tokens // blk, finish, 0)
@@ -246,8 +241,6 @@
         return 0
 
     lax.fori_loop(0, experts_here, drain, 0)
-    for t in range(tokens // blk):
-        out_copy(t).wait()
 
 
 def solution(mesh):
@@ -262,9 +255,9 @@
         vmem, dma = pltpu.VMEM, pltpu.SemaphoreType.DMA
         out = pl.pallas_call(
             functools.partial(layer_kernel, cap),
-            out_shape=jax.ShapeDtypeStruct((token_count, dim), bf16),
+            out_shape=pltpu.VMEM((token_count, dim), bf16),
             in_specs=[pl.BlockSpec(memory_space=pl.ANY)] * 6,
-            out_specs=pl.BlockSpec(memory_space=pl.ANY),
+            out_specs=pl.BlockSpec(memory_space=pltpu.VMEM),
             scratch_shapes=[
                 vmem((token_count, dim), bf16),
                 vmem((experts, dim), bf16),
@@ -283,12 +276,10 @@
                 vmem((2, hidden, dim), bf16),
                 vmem((here, token_count, rows), bf16),
                 vmem((token_count, dim), f32),
-                vmem((token_count, dim), bf16),
                 dma((4,)), dma((2,)), dma((2,)),
                 dma((here, groups)), dma((here, groups)), dma((here, groups)), dma((here, groups)),
-                dma((4,)),
             ],
-            compiler_params=pltpu.CompilerParams(collective_id=0, has_side_effects=True, vmem_limit_bytes=67043328),
+            compiler_params=pltpu.CompilerParams(collective_id=0, has_side_effects=True, vmem_limit_bytes=60 * 2**20),
             name="moe_layer",
         )(tokens[0], w_gate.T, expert_ids[0].T, keep_second, w_in, w_out)
         return out[None]

time: 104 us -> 101 us (0.971)
  local copies, waits for them, and re-layouts: 3.08 us -> 1.32 us
    unnamed x1, local copies, waits for them, and re-layouts: 3.08 us -> 1.32 us
where the time goes in v2:
time: 101 us
  Pallas kernels  100 us (99%)
  local copies, waits for them, and re-layouts  1.32 us (1%)
    pallas_call x1, Pallas kernels, local_layer(): pl.pallas_call(functools.partial(layer_kernel, cap), out_shape=pltpu.VMEM...  100 us

profile of v2, /device:TPU:0, one launch (start us, length us, event | category | flops | bytes accessed | tf_op | source)
XLA Modules:
  0.0 101.3 jit_solution(7672610502358129162)
XLA Ops:
  0.0 100.0 %moe_layer.1 = bf16[1024,1024]{1,0:T(8,128)(2,1)S(1)} custom-call(bf16[1024,1024]{1,0:T(8,128)(2,1)} %bitcast.7, bf16[32,1024]{1,0:T(8,128)(2,1)} %bitcast.8, s32[2,1024]{1,0:T(2,128)} %bitcast.9, s32[1,1024]{1,0:T(1,128)} %keep_hbm.1, bf16[4,1024,2816]{2,1,0:T(8,128)(2,1)} %win_hbm.1, bf16[4,2816,1024]{2,1,0:T(8,128)(2,1)} %wout_hbm.1), custom_call_target="tpu_custom_call" | custom-call | tf_op jit(solution)/shard_map/moe_layer/pallas_call | solution.py:256
  100.0 1.3 %copy.8 = bf16[1,1024,1024]{2,1,0:T(8,128)(2,1)} copy(bf16[1,1024,1024]{2,1,0:T(8,128)(2,1)S(1)} %bitcast.6) | data formatting | bytes 4194304

commit v3 on v2

--- a/solution.py
+++ b/solution.py
@@ -8,7 +8,8 @@
 from jax.sharding import PartitionSpec as P
 
 MESH = pl.DeviceIdType.MESH
-SEND_ORDER = (6, 7, 2, 4, 3, 5, 1)
+ORDER = (0, 1, 6, 7, 2, 4, 3, 5)
+SENDS = (2, 3, 4, 5, 6, 7, 1)
 
 
 def peer_of(me, k):
@@ -34,10 +35,6 @@
     rows = groups * cap
     f32, bf16 = jnp.float32, jnp.bfloat16
 
-    barrier = pltpu.get_barrier_semaphore()
-    for k in range(1, 8):
-        pl.semaphore_signal(barrier, inc=1, device_id={"ep": peer_of(me, k)}, device_id_type=MESH)
-
     small = [
         pltpu.make_async_copy(ids_hbm, ids, in_sem.at[0]),
         pltpu.make_async_copy(keep_hbm, keep, in_sem.at[1]),
@@ -47,15 +44,15 @@
     for copy in small:
         copy.start()
 
+    barrier = pltpu.get_barrier_semaphore()
+    for k in range(1, 8):
+        pl.semaphore_signal(barrier, inc=1, device_id={"ep": peer_of(me, k)}, device_id_type=MESH)
+
     def wi_copy(e):
         return pltpu.make_async_copy(win_hbm.at[e], wi.at[e % 2], wi_sem.at[e % 2])
 
     def wo_copy(e):
         return pltpu.make_async_copy(wout_hbm.at[e], wo.at[e % 2], wo_sem.at[e % 2])
-
-    for e in range(2):
-        wi_copy(e).start()
-        wo_copy(e).start()
 
     small[0].wait()
     small[1].wait()
@@ -84,31 +81,43 @@
     keys[0:1, :] = key1
     keys[1:2, :] = key2
 
-    def x_send(e, k):
-        peer = peer_of(me, k)
+    def send(src, dst, send_sem, recv_sem, e, p):
+        at = pl.ds(p * cap, cap)
         return pltpu.make_async_remote_copy(
-            src_ref=xs.at[e, pl.ds(pl.multiple_of(peer * cap, cap), cap)],
-            dst_ref=xr.at[e, pl.ds(pl.multiple_of(me * cap, cap), cap)],
-            send_sem=xs_sem.at[e, k], recv_sem=xr_sem.at[e, k],
-            device_id={"ep": peer}, device_id_type=MESH,
+            src_ref=src.at[e, at], dst_ref=dst.at[e, at],
+            send_sem=send_sem.at[e, p], recv_sem=recv_sem.at[e, p],
+            device_id={"ep": peer_of(me, ORDER[p])}, device_id_type=MESH,
         )
 
-    def y_send(e, k):
-        peer = peer_of(me, k)
-        return pltpu.make_async_remote_copy(
-            src_ref=ys.at[e, pl.ds(pl.multiple_of(peer * cap, cap), cap)],
-            dst_ref=yr.at[e, pl.ds(pl.multiple_of(me * cap, cap), cap)],
-            send_sem=ys_sem.at[e, k], recv_sem=yr_sem.at[e, k],
-            device_id={"ep": peer}, device_id_type=MESH,
-        )
-
-    mine = pl.ds(pl.multiple_of(me * cap, cap), cap)
-
-    def dispatch(e):
-        row = lax.broadcasted_iota(jnp.int32, (rows, tokens), 0)
-        slot = (row // cap) * (experts_here * cap) + e * cap + row % cap
+    x_send = functools.partial(send, xs, xr, xs_sem, xr_sem)
+    y_send = functools.partial(send, ys, yr, ys_sem, yr_sem)
+
+    def first_slot(e, p):
+        return peer_of(me, ORDER[p]) * (experts_here * cap) + e * cap
+
+    def pair_hot(e, q):
+        row = lax.broadcasted_iota(jnp.int32, (2 * cap, tokens), 0)
+        slot = row + jnp.where(row < cap, first_slot(e, 2 * q), first_slot(e, 2 * q + 1) - cap)
         hit = (slot == keys[0:1, :]) | (slot == keys[1:2, :])
-        dmat[...] = jnp.where(hit, 1.0, 0.0).astype(bf16)
+        return jnp.where(hit, 1.0, 0.0).astype(bf16)
+
+    small[2].wait()
+    for q in (1, 2, 3, 0):
+        at = pl.ds(q * 2 * cap, 2 * cap)
+        xs[0, at] = jnp.dot(pair_hot(0, q), tok[...], preferred_element_type=f32).astype(bf16)
+        if q == 1:
+            pl.semaphore_wait(barrier, 7)
+        for p in (2 * q, 2 * q + 1):
+            if p:
+                x_send(0, p).start()
+    xr[0, 0:cap] = xs[0, 0:cap]
+    for e in range(2):
+        wi_copy(e).start()
+        wo_copy(e).start()
+
+    def dispatch(e, _):
+        for q in range(groups // 2):
+            dmat[pl.ds(q * 2 * cap, 2 * cap), :] = pair_hot(e, q)
 
         def columns(n, _):
             at = pl.ds(pl.multiple_of(n * blk, blk), blk)
@@ -116,21 +125,12 @@
             return 0
 
         lax.fori_loop(0, dim // blk, columns, 0)
-        xr[e, mine] = xs[e, mine]
-
-    small[2].wait()
-    dispatch(0)
-    pl.semaphore_wait(barrier, 7)
-    for k in SEND_ORDER:
-        x_send(0, k).start()
-
-    def dispatch_rest(e, _):
-        dispatch(e)
-        for k in SEND_ORDER:
-            x_send(e, k).start()
-        return 0
-
-    lax.fori_loop(1, experts_here, dispatch_rest, 0)
+        for p in SENDS:
+            x_send(e, p).start()
+        xr[e, 0:cap] = xs[e, 0:cap]
+        return 0
+
+    lax.fori_loop(1, experts_here, dispatch, 0)
 
     small[3].wait()
     logits = lax.dot_general(wg[...], tok[...], (((1,), (1,)), ((), ())), preferred_element_type=f32)
@@ -150,8 +150,11 @@
     def weights(e, _):
         def block(t, _):
             at = pl.ds(pl.multiple_of(t * blk, blk), blk)
-            lane = lax.broadcasted_iota(jnp.int32, (blk, rows), 1)
-            slot = ((lane // cap) * (experts_here * cap) + e * cap + lane % cap).astype(f32)
+            lane = lax.broadcasted_iota(jnp.int32, (8, rows), 1)
+            slot = lane
+            for p in range(groups):
+                slot = slot + jnp.where(lane // cap == p, first_slot(e, p) - p * cap, 0)
+            slot = slot[0:1, :].astype(f32)
             part = cols[at, :]
             cw[e, at, :] = (
                 jnp.where(slot == part[:, 0:1], part[:, 2:3], 0.0) + jnp.where(slot == part[:, 1:2], part[:, 3:4], 0.0)
@@ -164,8 +167,8 @@
 
     def expert(e, _):
         s = e % 2
-        for k in SEND_ORDER:
-            x_send(e, k).wait_recv()
+        for p in SENDS:
+            x_send(e, p).wait_recv()
         wi_copy(e).wait()
 
         def up(j, _):
@@ -193,51 +196,57 @@
         def _():
             wo_copy(e + 2).start()
 
-        for k in SEND_ORDER:
-            y_send(e, k).start()
-        yr[e, mine] = ys[e, mine]
+        for p in SENDS:
+            y_send(e, p).start()
+        yr[e, 0:cap] = ys[e, 0:cap]
         return 0
 
     lax.fori_loop(0, experts_here, expert, 0)
-
-    def back(e):
-        for k in SEND_ORDER:
-            y_send(e, k).wait_recv()
-
-    back(0)
 
     def first_columns(n, _):
         at = pl.ds(pl.multiple_of(n * blk, blk), blk)
         acc[:, at] = jnp.dot(cw[0], yr[0, :, at], preferred_element_type=f32)
         return 0
 
+    def combine(e, _):
+        for p in SENDS:
+            y_send(e, p).wait_recv()
+
+        def columns(n, _):
+            at = pl.ds(pl.multiple_of(n * blk, blk), blk)
+            acc[:, at] += jnp.dot(cw[e], yr[e, :, at], preferred_element_type=f32)
+            return 0
+
+        return lax.fori_loop(0, dim // blk, columns, 0)
+
+    for p in SENDS:
+        y_send(0, p).wait_recv()
     lax.fori_loop(0, dim // blk, first_columns, 0)
-
-    def combine(e, _):
-        back(e)
-
-        def columns(n, _):
-            at = pl.ds(pl.multiple_of(n * blk, blk), blk)
-            acc[:, at] += jnp.dot(cw[e], yr[e, :, at], preferred_element_type=f32)
-            return 0
-
-        return lax.fori_loop(0, dim // blk, columns, 0)
-
     lax.fori_loop(1, experts_here - 1, combine, 0)
     last = experts_here - 1
-    back(last)
-
-    def finish(t, _):
-        at = pl.ds(pl.multiple_of(t * blk, blk), blk)
-        obuf[at, :] = (acc[at, :] + jnp.dot(cw[last, at, :], yr[last], preferred_element_type=f32)).astype(bf16)
-        return 0
-
-    lax.fori_loop(0, tokens // blk, finish, 0)
+    for q in range(groups // 2 - 1):
+        for p in (2 * q, 2 * q + 1):
+            if p:
+                y_send(last, p).wait_recv()
+        pair = pl.ds(q * 2 * cap, 2 * cap)
+
+        def pair_columns(n, _):
+            at = pl.ds(pl.multiple_of(n * blk, blk), blk)
+            acc[:, at] += jnp.dot(cw[last, :, pair], yr[last, pair, at], preferred_element_type=f32)
+            return 0
+
+        lax.fori_loop(0, dim // blk, pair_columns, 0)
+    for p in (groups - 2, groups - 1):
+        y_send(last, p).wait_recv()
+    pair = pl.ds(rows - 2 * cap, 2 * cap)
+    for t in range(tokens // blk):
+        at = pl.ds(t * blk, blk)
+        obuf[at, :] = (acc[at, :] + jnp.dot(cw[last, at, pair], yr[last, pair], preferred_element_type=f32)).astype(bf16)
 
     def drain(e, _):
-        for k in SEND_ORDER:
-            x_send(e, k).wait_send()
-            y_send(e, k).wait_send()
+        for p in SENDS:
+            x_send(e, p).wait_send()
+            y_send(e, p).wait_send()
         return 0
 
     lax.fori_loop(0, experts_here, drain, 0)

time: 101 us -> 99.2 us (0.982)
  Pallas kernels: 100 us -> 97.8 us
    pallas_call x1, Pallas kernels: 100 us -> 97.8 us  [local_layer(): pl.pallas_call(functools.partial(layer_kernel, cap), out_shape=pltpu.VMEM...]
where the time goes in v3:
time: 99.2 us; the launch traced here: 99.1 us
  Pallas kernels  97.8 us (99%)
  local copies, waits for them, and re-layouts  1.32 us (1%)
    pallas_call x1, Pallas kernels, local_layer(): pl.pallas_call(functools.partial(layer_kernel, cap), out_shape=pltpu.VMEM...  97.8 us

profile of v3, /device:TPU:0, one launch (start us, length us, event | category | flops | bytes accessed | tf_op | source)
XLA Modules:
  0.0 99.1 jit_solution(919072882866752305)
XLA Ops:
  0.0 97.8 %moe_layer.1 = bf16[1024,1024]{1,0:T(8,128)(2,1)S(1)} custom-call(bf16[1024,1024]{1,0:T(8,128)(2,1)} %bitcast.7, bf16[32,1024]{1,0:T(8,128)(2,1)} %bitcast.8, s32[2,1024]{1,0:T(2,128)} %bitcast.9, s32[1,1024]{1,0:T(1,128)} %keep_hbm.1, bf16[4,1024,2816]{2,1,0:T(8,128)(2,1)} %win_hbm.1, bf16[4,2816,1024]{2,1,0:T(8,128)(2,1)} %wout_hbm.1), custom_call_target="tpu_custom_call" | custom-call | tf_op jit(solution)/shard_map/moe_layer/pallas_call | solution.py:265
  97.8 1.3 %copy.8 = bf16[1,1024,1024]{2,1,0:T(8,128)(2,1)} copy(bf16[1,1024,1024]{2,1,0:T(8,128)(2,1)S(1)} %bitcast.6) | data formatting | bytes 4194304

commit v4 on v3

--- a/solution.py
+++ b/solution.py
@@ -10,6 +10,8 @@
 MESH = pl.DeviceIdType.MESH
 ORDER = (0, 1, 6, 7, 2, 4, 3, 5)
 SENDS = (2, 3, 4, 5, 6, 7, 1)
+X_PIECES = ((0, 1), (1, 1), (2, 2))
+Y_PIECES = ((0, 2), (2, 1), (3, 1))
 
 
 def peer_of(me, k):
@@ -22,8 +24,8 @@
 
 
 def layer_kernel(
-    cap, tok_hbm, wg_hbm, ids_hbm, keep_hbm, win_hbm, wout_hbm, obuf,
-    tok, wg, ids, keep, keys, gates, cols, dmat, xs, xr, ys, yr, hid, wi, wo, cw, acc,
+    cap, tok_hbm, wg_hbm, ids_hbm, keep_hbm, win_hbm, wout_hbm, acc, cw_end, y_end,
+    tok, wg, ids, keep, keys, gates, cols, dmat, xs, xr, ys, yr, hid, wi, wo, cw,
     in_sem, wi_sem, wo_sem, xs_sem, xr_sem, ys_sem, yr_sem,
 ):
     me = lax.axis_index("ep")
@@ -81,16 +83,16 @@
     keys[0:1, :] = key1
     keys[1:2, :] = key2
 
-    def send(src, dst, send_sem, recv_sem, e, p):
-        at = pl.ds(p * cap, cap)
+    def send(src, dst, send_sem, recv_sem, pieces, i, p):
+        at = pl.ds(*pieces[i])
         return pltpu.make_async_remote_copy(
-            src_ref=src.at[e, at], dst_ref=dst.at[e, at],
-            send_sem=send_sem.at[e, p], recv_sem=recv_sem.at[e, p],
+            src_ref=src.at[p, at], dst_ref=dst.at[p, at],
+            send_sem=send_sem.at[i, p], recv_sem=recv_sem.at[i, p],
             device_id={"ep": peer_of(me, ORDER[p])}, device_id_type=MESH,
         )
 
-    x_send = functools.partial(send, xs, xr, xs_sem, xr_sem)
-    y_send = functools.partial(send, ys, yr, ys_sem, yr_sem)
+    x_send = functools.partial(send, xs, xr, xs_sem, xr_sem, X_PIECES)
+    y_send = functools.partial(send, ys, yr, ys_sem, yr_sem, Y_PIECES)
 
     def first_slot(e, p):
         return peer_of(me, ORDER[p]) * (experts_here * cap) + e * cap
@@ -103,14 +105,17 @@
 
     small[2].wait()
     for q in (1, 2, 3, 0):
-        at = pl.ds(q * 2 * cap, 2 * cap)
-        xs[0, at] = jnp.dot(pair_hot(0, q), tok[...], preferred_element_type=f32).astype(bf16)
+        got = jnp.dot(pair_hot(0, q), tok[...], preferred_element_type=f32).astype(bf16)
+        for p, part in ((2 * q, got[:cap]), (2 * q + 1, got[cap:])):
+            if p:
+                xs[p, 0] = part
+            else:
+                xr[p, 0] = part
         if q == 1:
             pl.semaphore_wait(barrier, 7)
         for p in (2 * q, 2 * q + 1):
             if p:
                 x_send(0, p).start()
-    xr[0, 0:cap] = xs[0, 0:cap]
     for e in range(2):
         wi_copy(e).start()
         wo_copy(e).start()
@@ -121,13 +126,17 @@
 
         def columns(n, _):
             at = pl.ds(pl.multiple_of(n * blk, blk), blk)
-            xs[e, :, at] = jnp.dot(dmat[...], tok[:, at], preferred_element_type=f32).astype(bf16)
+            got = jnp.dot(dmat[...], tok[:, at], preferred_element_type=f32).astype(bf16)
+            xs[:, e, :, at] = got.reshape(groups, cap, blk)
             return 0
 
         lax.fori_loop(0, dim // blk, columns, 0)
-        for p in SENDS:
-            x_send(e, p).start()
-        xr[e, 0:cap] = xs[e, 0:cap]
+        for i, (start, count) in enumerate(X_PIECES[1:], 1):
+            @pl.when(e == start + count - 1)
+            def _():
+                for p in SENDS:
+                    x_send(i, p).start()
+        xr[0, e] = xs[0, e]
         return 0
 
     lax.fori_loop(1, experts_here, dispatch, 0)
@@ -167,13 +176,17 @@
 
     def expert(e, _):
         s = e % 2
-        for p in SENDS:
-            x_send(e, p).wait_recv()
+        for i, (start, _count) in enumerate(X_PIECES):
+            @pl.when(e == start)
+            def _():
+                for p in SENDS:
+                    x_send(i, p).wait_recv()
+
         wi_copy(e).wait()
 
         def up(j, _):
             at = pl.ds(pl.multiple_of(j * blk, blk), blk)
-            pre = jnp.dot(xr[e], wi[s, :, at], preferred_element_type=f32)
+            pre = jnp.dot(xr[:, e].reshape(rows, dim), wi[s, :, at], preferred_element_type=f32)
             hid[:, at] = jnp.maximum(pre, 0.0).astype(bf16)
             return 0
 
@@ -187,7 +200,8 @@
 
         def down(n, _):
             at = pl.ds(pl.multiple_of(n * blk, blk), blk)
-            ys[e, :, at] = jnp.dot(hid[...], wo[s, :, at], preferred_element_type=f32).astype(bf16)
+            got = jnp.dot(hid[...], wo[s, :, at], preferred_element_type=f32).astype(bf16)
+            ys[:, e, :, at] = got.reshape(groups, cap, blk)
             return 0
 
         lax.fori_loop(0, dim // blk, down, 0)
@@ -196,25 +210,30 @@
         def _():
             wo_copy(e + 2).start()
 
-        for p in SENDS:
-            y_send(e, p).start()
-        yr[e, 0:cap] = ys[e, 0:cap]
+        for i, (start, count) in enumerate(Y_PIECES):
+            @pl.when(e == start + count - 1)
+            def _():
+                for p in SENDS:
+                    y_send(i, p).start()
+        yr[0, e] = ys[0, e]
         return 0
 
     lax.fori_loop(0, experts_here, expert, 0)
 
     def first_columns(n, _):
         at = pl.ds(pl.multiple_of(n * blk, blk), blk)
-        acc[:, at] = jnp.dot(cw[0], yr[0, :, at], preferred_element_type=f32)
+        acc[:, at] = jnp.dot(cw[0], yr[:, 0, :, at].reshape(rows, blk), preferred_element_type=f32)
         return 0
 
     def combine(e, _):
-        for p in SENDS:
-            y_send(e, p).wait_recv()
+        @pl.when(e == Y_PIECES[1][0])
+        def _():
+            for p in SENDS:
+                y_send(1, p).wait_recv()
 
         def columns(n, _):
             at = pl.ds(pl.multiple_of(n * blk, blk), blk)
-            acc[:, at] += jnp.dot(cw[e], yr[e, :, at], preferred_element_type=f32)
+            acc[:, at] += jnp.dot(cw[e], yr[:, e, :, at].reshape(rows, blk), preferred_element_type=f32)
             return 0
 
         return lax.fori_loop(0, dim // blk, columns, 0)
@@ -227,29 +246,38 @@
     for q in range(groups // 2 - 1):
         for p in (2 * q, 2 * q + 1):
             if p:
-                y_send(last, p).wait_recv()
+                y_send(2, p).wait_recv()
         pair = pl.ds(q * 2 * cap, 2 * cap)
 
         def pair_columns(n, _):
             at = pl.ds(pl.multiple_of(n * blk, blk), blk)
-            acc[:, at] += jnp.dot(cw[last, :, pair], yr[last, pair, at], preferred_element_type=f32)
+            back = yr[2 * q:2 * q + 2, last, :, at].reshape(2 * cap, blk)
+            acc[:, at] += jnp.dot(cw[last, :, pair], back, preferred_element_type=f32)
             return 0
 
         lax.fori_loop(0, dim // blk, pair_columns, 0)
+    pair = pl.ds(rows - 2 * cap, 2 * cap)
+    cw_end[...] = cw[last, :, pair]
     for p in (groups - 2, groups - 1):
-        y_send(last, p).wait_recv()
-    pair = pl.ds(rows - 2 * cap, 2 * cap)
-    for t in range(tokens // blk):
+        y_send(2, p).wait_recv()
+    y_end[...] = yr[groups - 2:, last].reshape(2 * cap, dim)
+
+    for i in range(len(X_PIECES)):
+        for p in SENDS:
+            x_send(i, p).wait_send()
+            y_send(i, p).wait_send()
+
+
+def finish_kernel(acc, cw, y, out, buf, sem):
+    blk = buf.shape[0] // 4
+    copies = []
+    for t in range(4):
         at = pl.ds(t * blk, blk)
-        obuf[at, :] = (acc[at, :] + jnp.dot(cw[last, at, pair], yr[last, pair], preferred_element_type=f32)).astype(bf16)
-
-    def drain(e, _):
-        for p in SENDS:
-            x_send(e, p).wait_send()
-            y_send(e, p).wait_send()
-        return 0
-
-    lax.fori_loop(0, experts_here, drain, 0)
+        buf[at, :] = (acc[at, :] + jnp.dot(cw[at, :], y[...], preferred_element_type=jnp.float32)).astype(out.dtype)
+        copies.append(pltpu.make_async_copy(buf.at[at], out.at[at], sem.at[t]))
+        copies[-1].start()
+    for copy in copies:
+        copy.wait()
 
 
 def solution(mesh):
@@ -262,11 +290,11 @@
         rows = groups * cap
         f32, bf16 = jnp.float32, jnp.bfloat16
         vmem, dma = pltpu.VMEM, pltpu.SemaphoreType.DMA
-        out = pl.pallas_call(
+        acc, cw_end, y_end = pl.pallas_call(
             functools.partial(layer_kernel, cap),
-            out_shape=pltpu.VMEM((token_count, dim), bf16),
+            out_shape=(vmem((token_count, dim), f32), vmem((token_count, 2 * cap), bf16), vmem((2 * cap, dim), bf16)),
             in_specs=[pl.BlockSpec(memory_space=pl.ANY)] * 6,
-            out_specs=pl.BlockSpec(memory_space=pltpu.VMEM),
+            out_specs=[pl.BlockSpec(memory_space=vmem)] * 3,
             scratch_shapes=[
                 vmem((token_count, dim), bf16),
                 vmem((experts, dim), bf16),
@@ -276,21 +304,29 @@
                 vmem((128, token_count), f32),
                 vmem((token_count, 128), f32),
                 vmem((rows, token_count), bf16),
-                vmem((here, rows, dim), bf16),
-                vmem((here, rows, dim), bf16),
-                vmem((here, rows, dim), bf16),
-                vmem((here, rows, dim), bf16),
+                vmem((groups, here, cap, dim), bf16),
+                vmem((groups, here, cap, dim), bf16),
+                vmem((groups, here, cap, dim), bf16),
+                vmem((groups, here, cap, dim), bf16),
                 vmem((rows, hidden), bf16),
                 vmem((2, dim, hidden), bf16),
                 vmem((2, hidden, dim), bf16),
                 vmem((here, token_count, rows), bf16),
-                vmem((token_count, dim), f32),
                 dma((4,)), dma((2,)), dma((2,)),
-                dma((here, groups)), dma((here, groups)), dma((here, groups)), dma((here, groups)),
+                dma((3, groups)), dma((3, groups)), dma((3, groups)), dma((3, groups)),
             ],
-            compiler_params=pltpu.CompilerParams(collective_id=0, has_side_effects=True, vmem_limit_bytes=60 * 2**20),
+            compiler_params=pltpu.CompilerParams(collective_id=0, has_side_effects=True, vmem_limit_bytes=56 * 2**20),
             name="moe_layer",
         )(tokens[0], w_gate.T, expert_ids[0].T, keep_second, w_in, w_out)
+        out = pl.pallas_call(
+            finish_kernel,
+            out_shape=jax.ShapeDtypeStruct((token_count, dim), bf16),
+            in_specs=[pl.BlockSpec(memory_space=vmem)] * 3,
+            out_specs=pl.BlockSpec(memory_space=pl.ANY),
+            scratch_shapes=[vmem((token_count, dim), bf16), dma((4,))],
+            compiler_params=pltpu.CompilerParams(vmem_limit_bytes=8 * 2**20),
+            name="moe_finish",
+        )(acc, cw_end, y_end)
         return out[None]
 
     group_spec = P(("dp", "ep"))

time: 99.2 us -> 98.6 us (level)
  local copies, waits for them, and re-layouts: 1.32 us -> 0 us
    unnamed x1 -> x0, local copies, waits for them, and re-layouts: 1.32 us -> none
    pallas_call x1 -> x2, Pallas kernels: 97.8 us -> 98.4 us  [the longest x1 96.8 us: local_layer(): pl.pallas_call(functools.partial(layer_kernel, cap), out_shape=(vmem((tok...]
where the time goes in v4:
time: 98.6 us; the launch traced here: 98.4 us
  Pallas kernels  98.4 us (100%)
    pallas_call x1, Pallas kernels, local_layer(): pl.pallas_call(functools.partial(layer_kernel, cap), out_shape=(vmem((tok...  96.8 us

profile of v4, /device:TPU:0, one launch (start us, length us, event | category | flops | bytes accessed | tf_op | source)
XLA Modules:
  0.0 98.4 jit_solution(5961700051795078921)
XLA Ops:
  0.0 96.8 %moe_layer.1 = (f32[1024,1024]{1,0:T(8,128)S(1)}, bf16[1024,128]{1,0:T(8,128)(2,1)S(1)}, bf16[128,1024]{1,0:T(8,128)(2,1)S(1)}) custom-call(bf16[1024,1024]{1,0:T(8,128)(2,1)} %bitcast.6, bf16[32,1024]{1,0:T(8,128)(2,1)} %bitcast.7, s32[2,1024]{1,0:T(2,128)} %bitcast.8, s32[1,1024]{1,0:T(1,128)} %keep_hbm.1, bf16[4,1024,2816]{2,1,0:T(8,128)(2,1)} %win_hbm.1, ...), custom_call_target="tpu_custom_call" | custom-call | tf_op jit(solution)/shard_map/moe_layer/pallas_call | solution.py:293
  96.8 1.6 %moe_finish.1 = bf16[1024,1024]{1,0:T(8,128)(2,1)} custom-call(f32[1024,1024]{1,0:T(8,128)S(1)} %get-tuple-element.8.acc, bf16[1024,128]{1,0:T(8,128)(2,1)S(1)} %get-tuple-element.9.cw, bf16[128,1024]{1,0:T(8,128)(2,1)S(1)} %get-tuple-element.10.y), custom_call_target="tpu_custom_call" | custom-call | tf_op jit(solution)/shard_map/moe_finish/pallas_call | solution.py:321

commit v5 on v4

--- a/solution.py
+++ b/solution.py
@@ -11,7 +11,7 @@
 ORDER = (0, 1, 6, 7, 2, 4, 3, 5)
 SENDS = (2, 3, 4, 5, 6, 7, 1)
 X_PIECES = ((0, 1), (1, 1), (2, 2))
-Y_PIECES = ((0, 2), (2, 1), (3, 1))
+Y_PIECES = ((0, 2), (2, 2))
 
 
 def peer_of(me, k):
@@ -104,16 +104,19 @@
         return jnp.where(hit, 1.0, 0.0).astype(bf16)
 
     small[2].wait()
-    for q in (1, 2, 3, 0):
-        got = jnp.dot(pair_hot(0, q), tok[...], preferred_element_type=f32).astype(bf16)
-        for p, part in ((2 * q, got[:cap]), (2 * q + 1, got[cap:])):
+    for half in ((1, 2), (3, 0)):
+        for i, q in enumerate(half):
+            dmat[pl.ds(i * 2 * cap, 2 * cap), :] = pair_hot(0, q)
+        got = jnp.dot(dmat[0:4 * cap, :], tok[...], preferred_element_type=f32).astype(bf16)
+        blocks = [2 * q + side for q in half for side in (0, 1)]
+        for i, p in enumerate(blocks):
             if p:
-                xs[p, 0] = part
+                xs[p, 0] = got[i * cap:(i + 1) * cap]
             else:
-                xr[p, 0] = part
-        if q == 1:
+                xr[p, 0] = got[i * cap:(i + 1) * cap]
+        if half[0] == 1:
             pl.semaphore_wait(barrier, 7)
-        for p in (2 * q, 2 * q + 1):
+        for p in blocks:
             if p:
                 x_send(0, p).start()
     for e in range(2):
@@ -156,23 +159,23 @@
     gates[4:, :] = jnp.zeros((gates.shape[0] - 4, tokens), f32)
     cols[...] = gates[...].T
 
-    def weights(e, _):
+    def weights(i, _):
         def block(t, _):
             at = pl.ds(pl.multiple_of(t * blk, blk), blk)
-            lane = lax.broadcasted_iota(jnp.int32, (8, rows), 1)
+            lane = lax.broadcasted_iota(jnp.int32, (8, 2 * rows), 1)
             slot = lane
             for p in range(groups):
-                slot = slot + jnp.where(lane // cap == p, first_slot(e, p) - p * cap, 0)
+                slot = slot + jnp.where(lane // (2 * cap) == p, first_slot(2 * i, p) - p * 2 * cap, 0)
             slot = slot[0:1, :].astype(f32)
             part = cols[at, :]
-            cw[e, at, :] = (
+            cw[i, at, :] = (
                 jnp.where(slot == part[:, 0:1], part[:, 2:3], 0.0) + jnp.where(slot == part[:, 1:2], part[:, 3:4], 0.0)
             ).astype(bf16)
             return 0
 
         return lax.fori_loop(0, tokens // blk, block, 0)
 
-    lax.fori_loop(0, experts_here, weights, 0)
+    lax.fori_loop(0, experts_here // 2, weights, 0)
 
     def expert(e, _):
         s = e % 2
@@ -220,58 +223,44 @@
 
     lax.fori_loop(0, experts_here, expert, 0)
 
-    def first_columns(n, _):
-        at = pl.ds(pl.multiple_of(n * blk, blk), blk)
-        acc[:, at] = jnp.dot(cw[0], yr[:, 0, :, at].reshape(rows, blk), preferred_element_type=f32)
-        return 0
-
-    def combine(e, _):
-        @pl.when(e == Y_PIECES[1][0])
-        def _():
-            for p in SENDS:
-                y_send(1, p).wait_recv()
-
-        def columns(n, _):
-            at = pl.ds(pl.multiple_of(n * blk, blk), blk)
-            acc[:, at] += jnp.dot(cw[e], yr[:, e, :, at].reshape(rows, blk), preferred_element_type=f32)
-            return 0
-
-        return lax.fori_loop(0, dim // blk, columns, 0)
-
     for p in SENDS:
         y_send(0, p).wait_recv()
-    lax.fori_loop(0, dim // blk, first_columns, 0)
-    lax.fori_loop(1, experts_here - 1, combine, 0)
-    last = experts_here - 1
+
+    def columns(n, _):
+        at = pl.ds(pl.multiple_of(n * blk, blk), blk)
+        acc[:, at] = jnp.dot(cw[0], yr[:, 0:2, :, at].reshape(2 * rows, blk), preferred_element_type=f32)
+        return 0
+
+    lax.fori_loop(0, dim // blk, columns, 0)
     for q in range(groups // 2 - 1):
         for p in (2 * q, 2 * q + 1):
             if p:
-                y_send(2, p).wait_recv()
-        pair = pl.ds(q * 2 * cap, 2 * cap)
+                y_send(1, p).wait_recv()
 
         def pair_columns(n, _):
             at = pl.ds(pl.multiple_of(n * blk, blk), blk)
-            back = yr[2 * q:2 * q + 2, last, :, at].reshape(2 * cap, blk)
-            acc[:, at] += jnp.dot(cw[last, :, pair], back, preferred_element_type=f32)
+            back = yr[2 * q:2 * q + 2, 2:4, :, at].reshape(4 * cap, blk)
+            acc[:, at] += jnp.dot(cw[1, :, q * 4 * cap:(q + 1) * 4 * cap], back, preferred_element_type=f32)
             return 0
 
         lax.fori_loop(0, dim // blk, pair_columns, 0)
-    pair = pl.ds(rows - 2 * cap, 2 * cap)
-    cw_end[...] = cw[last, :, pair]
+    cw_end[...] = cw[1, :, 2 * rows - 4 * cap:]
     for p in (groups - 2, groups - 1):
-        y_send(2, p).wait_recv()
-    y_end[...] = yr[groups - 2:, last].reshape(2 * cap, dim)
+        y_send(1, p).wait_recv()
+    y_end[...] = yr[groups - 2:, 2:4].reshape(4 * cap, dim)
 
     for i in range(len(X_PIECES)):
         for p in SENDS:
             x_send(i, p).wait_send()
+    for i in range(len(Y_PIECES)):
+        for p in SENDS:
             y_send(i, p).wait_send()
 
 
 def finish_kernel(acc, cw, y, out, buf, sem):
-    blk = buf.shape[0] // 4
+    blk = buf.shape[0] // 8
     copies = []
-    for t in range(4):
+    for t in range(8):
         at = pl.ds(t * blk, blk)
         buf[at, :] = (acc[at, :] + jnp.dot(cw[at, :], y[...], preferred_element_type=jnp.float32)).astype(out.dtype)
         copies.append(pltpu.make_async_copy(buf.at[at], out.at[at], sem.at[t]))
@@ -292,7 +281,7 @@
         vmem, dma = pltpu.VMEM, pltpu.SemaphoreType.DMA
         acc, cw_end, y_end = pl.pallas_call(
             functools.partial(layer_kernel, cap),
-            out_shape=(vmem((token_count, dim), f32), vmem((token_count, 2 * cap), bf16), vmem((2 * cap, dim), bf16)),
+            out_shape=(vmem((token_count, dim), f32), vmem((token_count, 4 * cap), bf16), vmem((4 * cap, dim), bf16)),
             in_specs=[pl.BlockSpec(memory_space=pl.ANY)] * 6,
             out_specs=[pl.BlockSpec(memory_space=vmem)] * 3,
             scratch_shapes=[
@@ -311,9 +300,9 @@
                 vmem((rows, hidden), bf16),
                 vmem((2, dim, hidden), bf16),
                 vmem((2, hidden, dim), bf16),
-                vmem((here, token_count, rows), bf16),
+                vmem((here // 2, token_count, 2 * rows), bf16),
                 dma((4,)), dma((2,)), dma((2,)),
-                dma((3, groups)), dma((3, groups)), dma((3, groups)), dma((3, groups)),
+                dma((3, groups)), dma((3, groups)), dma((2, groups)), dma((2, groups)),
             ],
             compiler_params=pltpu.CompilerParams(collective_id=0, has_side_effects=True, vmem_limit_bytes=56 * 2**20),
             name="moe_layer",
@@ -323,7 +312,7 @@
             out_shape=jax.ShapeDtypeStruct((token_count, dim), bf16),
             in_specs=[pl.BlockSpec(memory_space=vmem)] * 3,
             out_specs=pl.BlockSpec(memory_space=pl.ANY),
-            scratch_shapes=[vmem((token_count, dim), bf16), dma((4,))],
+            scratch_shapes=[vmem((token_count, dim), bf16), dma((8,))],
             compiler_params=pltpu.CompilerParams(vmem_limit_bytes=8 * 2**20),
             name="moe_finish",
         )(acc, cw_end, y_end)

time: 98.6 us -> 98.2 us (level)
  no operation moved by 1% of the time
where the time goes in v5:
time: 98.2 us; the launch traced here: 98.1 us
  Pallas kernels  98.1 us (100%)
    pallas_call x1, Pallas kernels, local_layer(): pl.pallas_call(functools.partial(layer_kernel, cap), out_shape=(vmem((tok...  96.5 us

profile of v5, /device:TPU:0, one launch (start us, length us, event | category | flops | bytes accessed | tf_op | source)
XLA Modules:
  0.0 98.1 jit_solution(7560941061467659278)
XLA Ops:
  0.0 96.5 %moe_layer.1 = (f32[1024,1024]{1,0:T(8,128)S(1)}, bf16[1024,256]{1,0:T(8,128)(2,1)S(1)}, bf16[256,1024]{1,0:T(8,128)(2,1)S(1)}) custom-call(bf16[1024,1024]{1,0:T(8,128)(2,1)} %bitcast.6, bf16[32,1024]{1,0:T(8,128)(2,1)} %bitcast.7, s32[2,1024]{1,0:T(2,128)} %bitcast.8, s32[1,1024]{1,0:T(1,128)} %keep_hbm.1, bf16[4,1024,2816]{2,1,0:T(8,128)(2,1)} %win_hbm.1, ...), custom_call_target="tpu_custom_call" | custom-call | tf_op jit(solution)/shard_map/moe_layer/pallas_call | solution.py:282
  96.5 1.6 %moe_finish.1 = bf16[1024,1024]{1,0:T(8,128)(2,1)} custom-call(f32[1024,1024]{1,0:T(8,128)S(1)} %get-tuple-element.8.acc, bf16[1024,256]{1,0:T(8,128)(2,1)S(1)} %get-tuple-element.9.cw, bf16[256,1024]{1,0:T(8,128)(2,1)S(1)} %get-tuple-element.10.y), custom_call_target="tpu_custom_call" | custom-call | tf_op jit(solution)/shard_map/moe_finish/pallas_call | solution.py:310

commit v6 on v5

--- a/solution.py
+++ b/solution.py
@@ -25,7 +25,7 @@
 
 def layer_kernel(
     cap, tok_hbm, wg_hbm, ids_hbm, keep_hbm, win_hbm, wout_hbm, acc, cw_end, y_end,
-    tok, wg, ids, keep, keys, gates, cols, dmat, xs, xr, ys, yr, hid, wi, wo, cw,
+    tok, wg, ids, keep, slot_of, gates, cols, dmat, xs, xr, ys, yr, hid, wi, wo, cw,
     in_sem, wi_sem, wo_sem, xs_sem, xr_sem, ys_sem, yr_sem,
 ):
     me = lax.axis_index("ep")
@@ -37,12 +37,13 @@
     rows = groups * cap
     f32, bf16 = jnp.float32, jnp.bfloat16
 
+    parts = (pl.ds(0, dim // 2), pl.ds(dim // 2, dim // 2))
     small = [
         pltpu.make_async_copy(ids_hbm, ids, in_sem.at[0]),
         pltpu.make_async_copy(keep_hbm, keep, in_sem.at[1]),
-        pltpu.make_async_copy(tok_hbm, tok, in_sem.at[2]),
-        pltpu.make_async_copy(wg_hbm, wg, in_sem.at[3]),
-    ]
+    ] + [
+        pltpu.make_async_copy(tok_hbm.at[:, part], tok.at[:, part], in_sem.at[2 + i]) for i, part in enumerate(parts)
+    ] + [pltpu.make_async_copy(wg_hbm, wg, in_sem.at[4])]
     for copy in small:
         copy.start()
 
@@ -56,37 +57,35 @@
     def wo_copy(e):
         return pltpu.make_async_copy(wout_hbm.at[e], wo.at[e % 2], wo_sem.at[e % 2])
 
-    small[0].wait()
-    small[1].wait()
-    expert_row = lax.broadcasted_iota(jnp.int32, (experts, tokens), 0)
-    id1, id2, kept2 = ids[0:1, :], ids[1:2, :], keep[0:1, :]
-    hot1 = (expert_row == id1).astype(f32)
-    hot2 = ((expert_row == id2) & (kept2 > 0)).astype(f32)
-    hot = jnp.concatenate([hot1, hot2], axis=0).astype(bf16)
     blk = 256
     r_io = lax.broadcasted_iota(jnp.int32, (blk, blk), 0)
     c_io = lax.broadcasted_iota(jnp.int32, (blk, blk), 1)
     before = jnp.where(r_io < c_io, 1.0, 0.0).astype(bf16)
     ones = jnp.ones((blk, blk), bf16)
-    seen = jnp.zeros((2 * experts, blk), f32)
-    earlier = []
-    for b in range(tokens // blk):
-        part = hot[:, b * blk:(b + 1) * blk]
-        earlier.append(jnp.dot(part, before, preferred_element_type=f32) + seen)
-        seen = seen + jnp.dot(part, ones, preferred_element_type=f32)
-    first_total = seen[:experts, :]
-    pos1 = jnp.concatenate([jnp.sum(p[:experts] * hot1[:, b * blk:(b + 1) * blk], axis=0, keepdims=True) for b, p in enumerate(earlier)], axis=1)
-    pos2 = jnp.concatenate([jnp.sum((p[experts:] + first_total) * hot2[:, b * blk:(b + 1) * blk], axis=0, keepdims=True) for b, p in enumerate(earlier)], axis=1)
-    pos1, pos2 = pos1.astype(jnp.int32), pos2.astype(jnp.int32)
-    key1 = jnp.where(pos1 < cap, id1 * cap + pos1, -1)
-    key2 = jnp.where((pos2 < cap) & (kept2 > 0), id2 * cap + pos2, -1)
-    keys[0:1, :] = key1
-    keys[1:2, :] = key2
+    expert_row = lax.broadcasted_iota(jnp.int32, (experts, tokens), 0)
+    small[0].wait()
+    small[1].wait()
+    hot1 = (expert_row == ids[0:1, :]).astype(f32)
+    hot2 = ((expert_row == ids[1:2, :]) & (keep[0:1, :] > 0)).astype(f32)
+    hot = jnp.concatenate([hot1, hot2], axis=0).astype(bf16)
+    blocks = range(tokens // blk)
+    stack = jnp.concatenate([hot[:, b * blk:(b + 1) * blk] for b in blocks], axis=0)
+    within = jnp.dot(stack, before, preferred_element_type=f32)
+    counts = jnp.dot(stack, ones, preferred_element_type=f32)
+    both = 2 * experts
+    first_total = sum(counts[b * both:b * both + experts] for b in blocks)
+    seen = jnp.zeros((both, blk), f32)
+    for b in blocks:
+        at = slice(b * blk, (b + 1) * blk)
+        earlier = within[b * both:(b + 1) * both] + seen
+        seen = seen + counts[b * both:(b + 1) * both]
+        second = jnp.where(hot2[:, at] > 0, earlier[experts:] + first_total, -1.0)
+        slot_of[:, at] = jnp.where(hot1[:, at] > 0, earlier[:experts], second)
 
     def send(src, dst, send_sem, recv_sem, pieces, i, p):
         at = pl.ds(*pieces[i])
         return pltpu.make_async_remote_copy(
-            src_ref=src.at[p, at], dst_ref=dst.at[p, at],
+            src_ref=src.at[p, at], dst_ref=y_end.at[p - 6] if dst is yr and i == 1 and p >= 6 else dst.at[p, at],
             send_sem=send_sem.at[i, p], recv_sem=recv_sem.at[i, p],
             device_id={"ep": peer_of(me, ORDER[p])}, device_id_type=MESH,
         )
@@ -97,26 +96,24 @@
     def first_slot(e, p):
         return peer_of(me, ORDER[p]) * (experts_here * cap) + e * cap
 
-    def pair_hot(e, q):
-        row = lax.broadcasted_iota(jnp.int32, (2 * cap, tokens), 0)
-        slot = row + jnp.where(row < cap, first_slot(e, 2 * q), first_slot(e, 2 * q + 1) - cap)
-        hit = (slot == keys[0:1, :]) | (slot == keys[1:2, :])
-        return jnp.where(hit, 1.0, 0.0).astype(bf16)
-
-    small[2].wait()
+    def block_hot(e, p):
+        slot = lax.broadcasted_iota(jnp.int32, (cap, tokens), 0).astype(f32)
+        taken = slot_of[pl.ds(peer_of(me, ORDER[p]) * experts_here + e, 1), :]
+        return jnp.where(slot == taken, 1.0, 0.0).astype(bf16)
+
     for half in ((1, 2), (3, 0)):
-        for i, q in enumerate(half):
-            dmat[pl.ds(i * 2 * cap, 2 * cap), :] = pair_hot(0, q)
-        got = jnp.dot(dmat[0:4 * cap, :], tok[...], preferred_element_type=f32).astype(bf16)
-        blocks = [2 * q + side for q in half for side in (0, 1)]
-        for i, p in enumerate(blocks):
-            if p:
-                xs[p, 0] = got[i * cap:(i + 1) * cap]
-            else:
-                xr[p, 0] = got[i * cap:(i + 1) * cap]
+        places = [2 * q + side for q in half for side in (0, 1)]
+        for i, p in enumerate(places):
+            dmat[i * cap:(i + 1) * cap, :] = block_hot(0, p)
+        for n, part in enumerate(parts):
+            if half[0] == 1:
+                small[2 + n].wait()
+            got = jnp.dot(dmat[0:4 * cap, :], tok[:, part], preferred_element_type=f32).astype(bf16)
+            for i, p in enumerate(places):
+                (xs if p else xr)[p, 0, :, part] = got[i * cap:(i + 1) * cap]
         if half[0] == 1:
             pl.semaphore_wait(barrier, 7)
-        for p in blocks:
+        for p in places:
             if p:
                 x_send(0, p).start()
     for e in range(2):
@@ -124,8 +121,8 @@
         wo_copy(e).start()
 
     def dispatch(e, _):
-        for q in range(groups // 2):
-            dmat[pl.ds(q * 2 * cap, 2 * cap), :] = pair_hot(e, q)
+        for p in range(groups):
+            dmat[p * cap:(p + 1) * cap, :] = block_hot(e, p)
 
         def columns(n, _):
             at = pl.ds(pl.multiple_of(n * blk, blk), blk)
@@ -144,16 +141,22 @@
 
     lax.fori_loop(1, experts_here, dispatch, 0)
 
-    small[3].wait()
+    small[4].wait()
     logits = lax.dot_general(wg[...], tok[...], (((1,), (1,)), ((), ())), preferred_element_type=f32)
     top = jnp.max(logits, axis=0, keepdims=True)
     expd = jnp.exp(logits - top)
     probs = expd / jnp.sum(expd, axis=0, keepdims=True)
-    gate1 = jnp.sum(jnp.where(expert_row == ids[0:1, :], probs, 0.0), axis=0, keepdims=True)
-    gate2 = jnp.sum(jnp.where((expert_row == ids[1:2, :]) & (keep[0:1, :] > 0), probs, 0.0), axis=0, keepdims=True)
+    id1, id2, kept2 = ids[0:1, :], ids[1:2, :], keep[0:1, :] > 0
+    is1, is2 = expert_row == id1, (expert_row == id2) & kept2
+
+    def pick(mask, value):
+        return jnp.sum(jnp.where(mask, value, 0.0), axis=0, keepdims=True)
+
+    gate1, gate2 = pick(is1, probs), pick(is2, probs)
+    slot1, slot2 = pick(is1, slot_of[...]), pick(is2, slot_of[...])
     total = gate1 + gate2
-    gates[0:1, :] = keys[0:1, :].astype(f32)
-    gates[1:2, :] = keys[1:2, :].astype(f32)
+    gates[0:1, :] = jnp.where(slot1 < cap, id1.astype(f32) * cap + slot1, -1.0)
+    gates[1:2, :] = jnp.where((slot2 < cap) & kept2, id2.astype(f32) * cap + slot2, -1.0)
     gates[2:3, :] = gate1 / total
     gates[3:4, :] = gate2 / total
     gates[4:, :] = jnp.zeros((gates.shape[0] - 4, tokens), f32)
@@ -245,16 +248,15 @@
 
         lax.fori_loop(0, dim // blk, pair_columns, 0)
     cw_end[...] = cw[1, :, 2 * rows - 4 * cap:]
-    for p in (groups - 2, groups - 1):
-        y_send(1, p).wait_recv()
-    y_end[...] = yr[groups - 2:, 2:4].reshape(4 * cap, dim)
-
     for i in range(len(X_PIECES)):
         for p in SENDS:
             x_send(i, p).wait_send()
-    for i in range(len(Y_PIECES)):
-        for p in SENDS:
-            y_send(i, p).wait_send()
+    for p in SENDS:
+        y_send(0, p).wait_send()
+    for p in (groups - 2, groups - 1):
+        y_send(1, p).wait_recv()
+    for p in SENDS:
+        y_send(1, p).wait_send()
 
 
 def finish_kernel(acc, cw, y, out, buf, sem):
@@ -262,7 +264,7 @@
     copies = []
     for t in range(8):
         at = pl.ds(t * blk, blk)
-        buf[at, :] = (acc[at, :] + jnp.dot(cw[at, :], y[...], preferred_element_type=jnp.float32)).astype(out.dtype)
+        buf[at, :] = (acc[at, :] + jnp.dot(cw[at, :], y[...].reshape(cw.shape[1], acc.shape[1]), preferred_element_type=jnp.float32)).astype(out.dtype)
         copies.append(pltpu.make_async_copy(buf.at[at], out.at[at], sem.at[t]))
         copies[-1].start()
     for copy in copies:
@@ -281,7 +283,7 @@
         vmem, dma = pltpu.VMEM, pltpu.SemaphoreType.DMA
         acc, cw_end, y_end = pl.pallas_call(
             functools.partial(layer_kernel, cap),
-            out_shape=(vmem((token_count, dim), f32), vmem((token_count, 4 * cap), bf16), vmem((4 * cap, dim), bf16)),
+            out_shape=(vmem((token_count, dim), f32), vmem((token_count, 4 * cap), bf16), vmem((2, 2, cap, dim), bf16)),
             in_specs=[pl.BlockSpec(memory_space=pl.ANY)] * 6,
             out_specs=[pl.BlockSpec(memory_space=vmem)] * 3,
             scratch_shapes=[
@@ -289,7 +291,7 @@
                 vmem((experts, dim), bf16),
                 vmem((2, token_count), jnp.int32),
                 vmem((1, token_count), jnp.int32),
-                vmem((8, token_count), jnp.int32),
+                vmem((experts, token_count), f32),
                 vmem((128, token_count), f32),
                 vmem((token_count, 128), f32),
                 vmem((rows, token_count), bf16),
@@ -301,7 +303,7 @@
                 vmem((2, dim, hidden), bf16),
                 vmem((2, hidden, dim), bf16),
                 vmem((here // 2, token_count, 2 * rows), bf16),
-                dma((4,)), dma((2,)), dma((2,)),
+                dma((5,)), dma((2,)), dma((2,)),
                 dma((3, groups)), dma((3, groups)), dma((2, groups)), dma((2, groups)),
             ],
             compiler_params=pltpu.CompilerParams(collective_id=0, has_side_effects=True, vmem_limit_bytes=56 * 2**20),

time: 98.2 us -> 97.9 us (level)
  no operation moved by 1% of the time
where the time goes in v6:
time: 97.9 us; the launch traced here: 97.8 us
  Pallas kernels  97.7 us (100%)
    pallas_call x1, Pallas kernels, local_layer(): pl.pallas_call(functools.partial(layer_kernel, cap), out_shape=(vmem((tok...  96.1 us

profile of v6, /device:TPU:0, one launch (start us, length us, event | category | flops | bytes accessed | tf_op | source)
XLA Modules:
  0.0 97.8 jit_solution(16948507548697119670)
XLA Ops:
  0.0 96.1 %moe_layer.1 = (f32[1024,1024]{1,0:T(8,128)S(1)}, bf16[1024,256]{1,0:T(8,128)(2,1)S(1)}, bf16[2,2,64,1024]{3,2,1,0:T(8,128)(2,1)S(1)}) custom-call(bf16[1024,1024]{1,0:T(8,128)(2,1)} %bitcast.6, bf16[32,1024]{1,0:T(8,128)(2,1)} %bitcast.7, s32[2,1024]{1,0:T(2,128)} %bitcast.8, s32[1,1024]{1,0:T(1,128)} %keep_hbm.1, bf16[4,1024,2816]{2,1,0:T(8,128)(2,1)} %win_hbm.1, ...), custom_call_target="tpu_custom_call" | custom-call | tf_op jit(solution)/shard_map/moe_layer/pallas_call | solution.py:284
  96.1 1.6 %moe_finish.1 = bf16[1024,1024]{1,0:T(8,128)(2,1)} custom-call(f32[1024,1024]{1,0:T(8,128)S(1)} %get-tuple-element.8.acc, bf16[1024,256]{1,0:T(8,128)(2,1)S(1)} %get-tuple-element.9.cw, bf16[2,2,64,1024]{3,2,1,0:T(8,128)(2,1)S(1)} %get-tuple-element.10.y), custom_call_target="tpu_custom_call" | custom-call | tf_op jit(solution)/shard_map/moe_finish/pallas_call | solution.py:312

commit v7 on v6

--- a/solution.py
+++ b/solution.py
@@ -82,16 +82,29 @@
         second = jnp.where(hot2[:, at] > 0, earlier[experts:] + first_total, -1.0)
         slot_of[:, at] = jnp.where(hot1[:, at] > 0, earlier[:experts], second)
 
-    def send(src, dst, send_sem, recv_sem, pieces, i, p):
-        at = pl.ds(*pieces[i])
+    def copy_to(p, src, dst, send_sem, recv_sem):
         return pltpu.make_async_remote_copy(
-            src_ref=src.at[p, at], dst_ref=y_end.at[p - 6] if dst is yr and i == 1 and p >= 6 else dst.at[p, at],
-            send_sem=send_sem.at[i, p], recv_sem=recv_sem.at[i, p],
+            src_ref=src, dst_ref=dst, send_sem=send_sem, recv_sem=recv_sem,
             device_id={"ep": peer_of(me, ORDER[p])}, device_id_type=MESH,
         )
 
-    x_send = functools.partial(send, xs, xr, xs_sem, xr_sem, X_PIECES)
-    y_send = functools.partial(send, ys, yr, ys_sem, yr_sem, Y_PIECES)
+    def x_send(i, p):
+        at = pl.ds(*X_PIECES[i])
+        return copy_to(p, xs.at[p, at], xr.at[p, at], xs_sem.at[0], xr_sem.at[i])
+
+    def x_wait(i):
+        at, places = pl.ds(*X_PIECES[i]), pl.ds(1, groups - 1)
+        copy_to(1, xs.at[places, at], xr.at[places, at], xs_sem.at[0], xr_sem.at[i]).wait_recv()
+
+    def y_send(i, p):
+        at = pl.ds(*Y_PIECES[i])
+        to = y_end.at[p - 6] if i == 1 and p >= 6 else yr.at[p, at]
+        return copy_to(p, ys.at[p, at], to, ys_sem.at[0], yr_sem.at[1 + p // 2 if i else 0])
+
+    def y_wait(i, first, count):
+        at, places = pl.ds(*Y_PIECES[i]), pl.ds(first, count)
+        to = y_end if i == 1 and first >= 6 else yr.at[places, at]
+        copy_to(1, ys.at[places, at], to, ys_sem.at[0], yr_sem.at[1 + first // 2 if i else 0]).wait_recv()
 
     def first_slot(e, p):
         return peer_of(me, ORDER[p]) * (experts_here * cap) + e * cap
@@ -185,8 +198,7 @@
         for i, (start, _count) in enumerate(X_PIECES):
             @pl.when(e == start)
             def _():
-                for p in SENDS:
-                    x_send(i, p).wait_recv()
+                x_wait(i)
 
         wi_copy(e).wait()
 
@@ -226,8 +238,7 @@
 
     lax.fori_loop(0, experts_here, expert, 0)
 
-    for p in SENDS:
-        y_send(0, p).wait_recv()
+    y_wait(0, 1, groups - 1)
 
     def columns(n, _):
         at = pl.ds(pl.multiple_of(n * blk, blk), blk)
@@ -236,9 +247,7 @@
 
     lax.fori_loop(0, dim // blk, columns, 0)
     for q in range(groups // 2 - 1):
-        for p in (2 * q, 2 * q + 1):
-            if p:
-                y_send(1, p).wait_recv()
+        y_wait(1, max(2 * q, 1), 2 if q else 1)
 
         def pair_columns(n, _):
             at = pl.ds(pl.multiple_of(n * blk, blk), blk)
@@ -248,27 +257,19 @@
 
         lax.fori_loop(0, dim // blk, pair_columns, 0)
     cw_end[...] = cw[1, :, 2 * rows - 4 * cap:]
-    for i in range(len(X_PIECES)):
-        for p in SENDS:
-            x_send(i, p).wait_send()
-    for p in SENDS:
-        y_send(0, p).wait_send()
-    for p in (groups - 2, groups - 1):
-        y_send(1, p).wait_recv()
-    for p in SENDS:
-        y_send(1, p).wait_send()
+    sent = pl.ds(1, groups - 1)
+    copy_to(1, xs.at[sent], xr.at[sent], xs_sem.at[0], xr_sem.at[0]).wait_send()
+    y_wait(1, groups - 2, 2)
+    copy_to(1, ys.at[sent], yr.at[sent], ys_sem.at[0], yr_sem.at[0]).wait_send()
 
 
 def finish_kernel(acc, cw, y, out, buf, sem):
     blk = buf.shape[0] // 8
-    copies = []
     for t in range(8):
         at = pl.ds(t * blk, blk)
         buf[at, :] = (acc[at, :] + jnp.dot(cw[at, :], y[...].reshape(cw.shape[1], acc.shape[1]), preferred_element_type=jnp.float32)).astype(out.dtype)
-        copies.append(pltpu.make_async_copy(buf.at[at], out.at[at], sem.at[t]))
-        copies[-1].start()
-    for copy in copies:
-        copy.wait()
+        pltpu.make_async_copy(buf.at[at], out.at[at], sem.at[0]).start()
+    pltpu.make_async_copy(buf, out, sem.at[0]).wait()
 
 
 def solution(mesh):
@@ -304,7 +305,7 @@
                 vmem((2, hidden, dim), bf16),
                 vmem((here // 2, token_count, 2 * rows), bf16),
                 dma((5,)), dma((2,)), dma((2,)),
-                dma((3, groups)), dma((3, groups)), dma((2, groups)), dma((2, groups)),
+                dma((1,)), dma((3,)), dma((1,)), dma((5,)),
             ],
             compiler_params=pltpu.CompilerParams(collective_id=0, has_side_effects=True, vmem_limit_bytes=56 * 2**20),
             name="moe_layer",
@@ -314,7 +315,7 @@
             out_shape=jax.ShapeDtypeStruct((token_count, dim), bf16),
             in_specs=[pl.BlockSpec(memory_space=vmem)] * 3,
             out_specs=pl.BlockSpec(memory_space=pl.ANY),
-            scratch_shapes=[vmem((token_count, dim), bf16), dma((8,))],
+            scratch_shapes=[vmem((token_count, dim), bf16), dma((1,))],
             compiler_params=pltpu.CompilerParams(vmem_limit_bytes=8 * 2**20),
             name="moe_finish",
         )(acc, cw_end, y_end)

time: 97.9 us -> 97.2 us (level)
  no operation moved by 1% of the time
where the time goes in v7:
time: 97.2 us; the launch traced here: 97.1 us
  Pallas kernels  97 us (100%)
    pallas_call x1, Pallas kernels, local_layer(): pl.pallas_call(functools.partial(layer_kernel, cap), out_shape=(vmem((tok...  95.5 us

profile of v7, /device:TPU:0, one launch (start us, length us, event | category | flops | bytes accessed | tf_op | source)
XLA Modules:
  0.0 97.1 jit_solution(3163972540009525183)
XLA Ops:
  0.0 95.5 %moe_layer.1 = (f32[1024,1024]{1,0:T(8,128)S(1)}, bf16[1024,256]{1,0:T(8,128)(2,1)S(1)}, bf16[2,2,64,1024]{3,2,1,0:T(8,128)(2,1)S(1)}) custom-call(bf16[1024,1024]{1,0:T(8,128)(2,1)} %bitcast.6, bf16[32,1024]{1,0:T(8,128)(2,1)} %bitcast.7, s32[2,1024]{1,0:T(2,128)} %bitcast.8, s32[1,1024]{1,0:T(1,128)} %keep_hbm.1, bf16[4,1024,2816]{2,1,0:T(8,128)(2,1)} %win_hbm.1, ...), custom_call_target="tpu_custom_call" | custom-call | tf_op jit(solution)/shard_map/moe_layer/pallas_call | solution.py:285
  95.5 1.6 %moe_finish.1 = bf16[1024,1024]{1,0:T(8,128)(2,1)} custom-call(f32[1024,1024]{1,0:T(8,128)S(1)} %get-tuple-element.8.acc, bf16[1024,256]{1,0:T(8,128)(2,1)S(1)} %get-tuple-element.9.cw, bf16[2,2,64,1024]{3,2,1,0:T(8,128)(2,1)S(1)} %get-tuple-element.10.y), custom_call_target="tpu_custom_call" | custom-call | tf_op jit(solution)/shard_map/moe_finish/pallas_call | solution.py:313

commit v8 on v7

--- a/solution.py
+++ b/solution.py
@@ -11,7 +11,13 @@
 ORDER = (0, 1, 6, 7, 2, 4, 3, 5)
 SENDS = (2, 3, 4, 5, 6, 7, 1)
 X_PIECES = ((0, 1), (1, 1), (2, 2))
-Y_PIECES = ((0, 2), (2, 2))
+Y_PIECES = ((0, 2), (2, 1), (2, 2))
+NEAR, FAR = (4, 5, 6, 7), (2, 3, 1)
+HELD = 16
+CW_BLOCKS = (
+    tuple((p, e) for p in range(8) for e in (0, 1)),
+    tuple((p, e) for p in range(4) for e in (2, 3)) + tuple((p, e) for e in (2, 3) for p in NEAR),
+)
 
 
 def peer_of(me, k):
@@ -25,7 +31,7 @@
 
 def layer_kernel(
     cap, tok_hbm, wg_hbm, ids_hbm, keep_hbm, win_hbm, wout_hbm, acc, cw_end, y_end,
-    tok, wg, ids, keep, slot_of, gates, cols, dmat, xs, xr, ys, yr, hid, wi, wo, cw,
+    tok, wg, ids, keep, slot_of, gates, cols, slots, dmat, xs, xr, ys, yr, hid, wi, wo, cw,
     in_sem, wi_sem, wo_sem, xs_sem, xr_sem, ys_sem, yr_sem,
 ):
     me = lax.axis_index("ep")
@@ -98,13 +104,15 @@
 
     def y_send(i, p):
         at = pl.ds(*Y_PIECES[i])
-        to = y_end.at[p - 6] if i == 1 and p >= 6 else yr.at[p, at]
-        return copy_to(p, ys.at[p, at], to, ys_sem.at[0], yr_sem.at[1 + p // 2 if i else 0])
+        return copy_to(p, ys.at[p, at], yr.at[p, at], ys_sem.at[0], yr_sem.at[(0, 1, 2 + p // 2)[i]])
 
     def y_wait(i, first, count):
         at, places = pl.ds(*Y_PIECES[i]), pl.ds(first, count)
-        to = y_end if i == 1 and first >= 6 else yr.at[places, at]
-        copy_to(1, ys.at[places, at], to, ys_sem.at[0], yr_sem.at[1 + first // 2 if i else 0]).wait_recv()
+        copy_to(1, ys.at[places, at], yr.at[places, at], ys_sem.at[0], yr_sem.at[(0, 1, 2 + first // 2)[i]]).wait_recv()
+
+    def end_send(p, first, count):
+        at = pl.ds(first, count)
+        return copy_to(p, ys.at[p, experts_here - 1, at], y_end.at[p - 4, at], ys_sem.at[0], yr_sem.at[4])
 
     def first_slot(e, p):
         return peer_of(me, ORDER[p]) * (experts_here * cap) + e * cap
@@ -175,14 +183,17 @@
     gates[4:, :] = jnp.zeros((gates.shape[0] - 4, tokens), f32)
     cols[...] = gates[...].T
 
+    for i, order in enumerate(CW_BLOCKS):
+        lane = lax.broadcasted_iota(jnp.int32, (8, 2 * rows), 1)
+        slot = lane
+        for b, (p, e) in enumerate(order):
+            slot = slot + jnp.where(lane // cap == b, first_slot(e, p) - b * cap, 0)
+        slots[i] = slot.astype(f32)
+
     def weights(i, _):
         def block(t, _):
             at = pl.ds(pl.multiple_of(t * blk, blk), blk)
-            lane = lax.broadcasted_iota(jnp.int32, (8, 2 * rows), 1)
-            slot = lane
-            for p in range(groups):
-                slot = slot + jnp.where(lane // (2 * cap) == p, first_slot(2 * i, p) - p * 2 * cap, 0)
-            slot = slot[0:1, :].astype(f32)
+            slot = slots[i, 0:1, :]
             part = cols[at, :]
             cw[i, at, :] = (
                 jnp.where(slot == part[:, 0:1], part[:, 2:3], 0.0) + jnp.where(slot == part[:, 1:2], part[:, 3:4], 0.0)
@@ -228,11 +239,31 @@
         def _():
             wo_copy(e + 2).start()
 
-        for i, (start, count) in enumerate(Y_PIECES):
-            @pl.when(e == start + count - 1)
-            def _():
-                for p in SENDS:
-                    y_send(i, p).start()
+        @pl.when(e == 1)
+        def _():
+            for p in SENDS:
+                y_send(0, p).start()
+
+        @pl.when(e == 2)
+        def _():
+            for p in NEAR:
+                y_send(1, p).start()
+
+        @pl.when(e == 3)
+        def _():
+            for p in FAR:
+                y_send(2, p).start()
+
+        @pl.when((e == 3) & (me % 2 == 0))
+        def _():
+            for p in NEAR:
+                end_send(p, 0, cap).start()
+
+        @pl.when((e == 3) & (me % 2 == 1))
+        def _():
+            for p, first, count in [(p, 0, cap - HELD) for p in (4, 5)] + [(p, 0, cap) for p in (6, 7)] + [(p, cap - HELD, HELD) for p in (4, 5)]:
+                end_send(p, first, count).start()
+
         yr[0, e] = ys[0, e]
         return 0
 
@@ -246,20 +277,24 @@
         return 0
 
     lax.fori_loop(0, dim // blk, columns, 0)
-    for q in range(groups // 2 - 1):
-        y_wait(1, max(2 * q, 1), 2 if q else 1)
-
-        def pair_columns(n, _):
+    def add_rows(first, back_of):
+        def part(n, _):
             at = pl.ds(pl.multiple_of(n * blk, blk), blk)
-            back = yr[2 * q:2 * q + 2, 2:4, :, at].reshape(4 * cap, blk)
-            acc[:, at] += jnp.dot(cw[1, :, q * 4 * cap:(q + 1) * 4 * cap], back, preferred_element_type=f32)
-            return 0
-
-        lax.fori_loop(0, dim // blk, pair_columns, 0)
+            acc[:, at] += jnp.dot(cw[1, :, first:first + 4 * cap], back_of(at).reshape(4 * cap, blk), preferred_element_type=f32)
+            return 0
+
+        lax.fori_loop(0, dim // blk, part, 0)
+
+    y_wait(1, 4, 4)
+    add_rows(rows, lambda at: yr[4:8, 2, :, at])
+    y_wait(2, 1, 1)
+    add_rows(0, lambda at: yr[0:2, 2:4, :, at])
+    y_wait(2, 2, 2)
+    add_rows(4 * cap, lambda at: yr[2:4, 2:4, :, at])
     cw_end[...] = cw[1, :, 2 * rows - 4 * cap:]
     sent = pl.ds(1, groups - 1)
     copy_to(1, xs.at[sent], xr.at[sent], xs_sem.at[0], xr_sem.at[0]).wait_send()
-    y_wait(1, groups - 2, 2)
+    copy_to(1, ys.at[4:8, 0], y_end, ys_sem.at[0], yr_sem.at[4]).wait_recv()
     copy_to(1, ys.at[sent], yr.at[sent], ys_sem.at[0], yr_sem.at[0]).wait_send()
 
 
@@ -284,7 +319,7 @@
         vmem, dma = pltpu.VMEM, pltpu.SemaphoreType.DMA
         acc, cw_end, y_end = pl.pallas_call(
             functools.partial(layer_kernel, cap),
-            out_shape=(vmem((token_count, dim), f32), vmem((token_count, 4 * cap), bf16), vmem((2, 2, cap, dim), bf16)),
+            out_shape=(vmem((token_count, dim), f32), vmem((token_count, 4 * cap), bf16), vmem((4, cap, dim), bf16)),
             in_specs=[pl.BlockSpec(memory_space=pl.ANY)] * 6,
             out_specs=[pl.BlockSpec(memory_space=vmem)] * 3,
             scratch_shapes=[
@@ -295,6 +330,7 @@
                 vmem((experts, token_count), f32),
                 vmem((128, token_count), f32),
                 vmem((token_count, 128), f32),
+                vmem((2, 8, 2 * rows), f32),
                 vmem((rows, token_count), bf16),
                 vmem((groups, here, cap, dim), bf16),
                 vmem((groups, here, cap, dim), bf16),

time: 97.2 us -> 97 us (level)
  no operation moved by 1% of the time
where the time goes in v8:
time: 97 us; the launch traced here: 96.6 us
  Pallas kernels  96.5 us (99%)
    pallas_call x1, Pallas kernels, local_layer(): pl.pallas_call(functools.partial(layer_kernel, cap), out_shape=(vmem((tok...  95 us

profile of v8, /device:TPU:0, one launch (start us, length us, event | category | flops | bytes accessed | tf_op | source)
XLA Modules:
  0.0 96.6 jit_solution(1681760925589681916)
XLA Ops:
  0.0 95.0 %moe_layer.1 = (f32[1024,1024]{1,0:T(8,128)S(1)}, bf16[1024,256]{1,0:T(8,128)(2,1)S(1)}, bf16[4,64,1024]{2,1,0:T(8,128)(2,1)S(1)}) custom-call(bf16[1024,1024]{1,0:T(8,128)(2,1)} %bitcast.6, bf16[32,1024]{1,0:T(8,128)(2,1)} %bitcast.7, s32[2,1024]{1,0:T(2,128)} %bitcast.8, s32[1,1024]{1,0:T(1,128)} %keep_hbm.1, bf16[4,1024,2816]{2,1,0:T(8,128)(2,1)} %win_hbm.1, ...), custom_call_target="tpu_custom_call" | custom-call | tf_op jit(solution)/shard_map/moe_layer/pallas_call | solution.py:320
  95.0 1.6 %moe_finish.1 = bf16[1024,1024]{1,0:T(8,128)(2,1)} custom-call(f32[1024,1024]{1,0:T(8,128)S(1)} %get-tuple-element.8.acc, bf16[1024,256]{1,0:T(8,128)(2,1)S(1)} %get-tuple-element.9.cw, bf16[4,64,1024]{2,1,0:T(8,128)(2,1)S(1)} %get-tuple-element.10.y), custom_call_target="tpu_custom_call" | custom-call | tf_op jit(solution)/shard_map/moe_finish/pallas_call | solution.py:349

commit v9 on v8

--- a/solution.py
+++ b/solution.py
@@ -14,6 +14,7 @@
 Y_PIECES = ((0, 2), (2, 1), (2, 2))
 NEAR, FAR = (4, 5, 6, 7), (2, 3, 1)
 HELD = 16
+HOP = 16
 CW_BLOCKS = (
     tuple((p, e) for p in range(8) for e in (0, 1)),
     tuple((p, e) for p in range(4) for e in (2, 3)) + tuple((p, e) for e in (2, 3) for p in NEAR),
@@ -31,8 +32,8 @@
 
 def layer_kernel(
     cap, tok_hbm, wg_hbm, ids_hbm, keep_hbm, win_hbm, wout_hbm, acc, cw_end, y_end,
-    tok, wg, ids, keep, slot_of, gates, cols, slots, dmat, xs, xr, ys, yr, hid, wi, wo, cw,
-    in_sem, wi_sem, wo_sem, xs_sem, xr_sem, ys_sem, yr_sem,
+    tok, wg, ids, keep, slot_of, gates, cols, slots, hop, dmat, xs, xr, ys, yr, hid, wi, wo, cw,
+    in_sem, wi_sem, wo_sem, xs_sem, xr_sem, ys_sem, yr_sem, hop_sem,
 ):
     me = lax.axis_index("ep")
     experts_here = win_hbm.shape[0]
@@ -98,6 +99,16 @@
         at = pl.ds(*X_PIECES[i])
         return copy_to(p, xs.at[p, at], xr.at[p, at], xs_sem.at[0], xr_sem.at[i])
 
+    def far_send(e, first, count):
+        at = pl.ds(first, count)
+        return copy_to(2, xs.at[2, e, at], xr.at[2, e, at], xs_sem.at[0], xr_sem.at[2])
+
+    def hop_send(e):
+        return copy_to(5, xs.at[2, e, pl.ds(cap - HOP, HOP)], hop, xs_sem.at[0], hop_sem.at[0])
+
+    def hop_on(e):
+        return copy_to(4, hop, xr.at[2, e, pl.ds(cap - HOP, HOP)], hop_sem.at[1], xr_sem.at[2])
+
     def x_wait(i):
         at, places = pl.ds(*X_PIECES[i]), pl.ds(1, groups - 1)
         copy_to(1, xs.at[places, at], xr.at[places, at], xs_sem.at[0], xr_sem.at[i]).wait_recv()
@@ -152,11 +163,27 @@
             return 0
 
         lax.fori_loop(0, dim // blk, columns, 0)
-        for i, (start, count) in enumerate(X_PIECES[1:], 1):
-            @pl.when(e == start + count - 1)
+        @pl.when(e == 1)
+        def _():
+            for p in SENDS:
+                x_send(1, p).start()
+
+        @pl.when(e == 3)
+        def _():
+            @pl.when(me == 3)
             def _():
-                for p in SENDS:
-                    x_send(i, p).start()
+                hop_send(3).start()
+                far_send(2, 0, cap).start()
+                if HOP < cap:
+                    far_send(3, 0, cap - HOP).start()
+
+            @pl.when(me != 3)
+            def _():
+                x_send(2, 2).start()
+
+            for p in SENDS[1:]:
+                x_send(2, p).start()
+
         xr[0, e] = xs[0, e]
         return 0
 
@@ -213,6 +240,11 @@
 
         wi_copy(e).wait()
 
+        @pl.when((e == 1) & (me == 7))
+        def _():
+            hop_send(3).wait_recv()
+            hop_on(3).start()
+
         def up(j, _):
             at = pl.ds(pl.multiple_of(j * blk, blk), blk)
             pre = jnp.dot(xr[:, e].reshape(rows, dim), wi[s, :, at], preferred_element_type=f32)
@@ -292,6 +324,10 @@
     y_wait(2, 2, 2)
     add_rows(4 * cap, lambda at: yr[2:4, 2:4, :, at])
     cw_end[...] = cw[1, :, 2 * rows - 4 * cap:]
+    @pl.when(me == 7)
+    def _():
+        hop_on(3).wait_send()
+
     sent = pl.ds(1, groups - 1)
     copy_to(1, xs.at[sent], xr.at[sent], xs_sem.at[0], xr_sem.at[0]).wait_send()
     copy_to(1, ys.at[4:8, 0], y_end, ys_sem.at[0], yr_sem.at[4]).wait_recv()
@@ -331,6 +367,7 @@
                 vmem((128, token_count), f32),
                 vmem((token_count, 128), f32),
                 vmem((2, 8, 2 * rows), f32),
+                vmem((HOP, dim), bf16),
                 vmem((rows, token_count), bf16),
                 vmem((groups, here, cap, dim), bf16),
                 vmem((groups, here, cap, dim), bf16),
@@ -341,7 +378,7 @@
                 vmem((2, hidden, dim), bf16),
                 vmem((here // 2, token_count, 2 * rows), bf16),
                 dma((5,)), dma((2,)), dma((2,)),
-                dma((1,)), dma((3,)), dma((1,)), dma((5,)),
+                dma((1,)), dma((3,)), dma((1,)), dma((5,)), dma((2,)),
             ],
             compiler_params=pltpu.CompilerParams(collective_id=0, has_side_effects=True, vmem_limit_bytes=56 * 2**20),
             name="moe_layer",

time: 97 us -> 96.7 us (level)
  no operation moved by 1% of the time
where the time goes in v9:
time: 96.7 us; the launch traced here: 96.6 us
  Pallas kernels  96.6 us (100%)
    pallas_call x1, Pallas kernels, local_layer(): pl.pallas_call(functools.partial(layer_kernel, cap), out_shape=(vmem((tok...  95 us

profile of v9, /device:TPU:0, one launch (start us, length us, event | category | flops | bytes accessed | tf_op | source)
XLA Modules:
  0.0 96.6 jit_solution(6500635223381056731)
XLA Ops:
  0.0 95.0 %moe_layer.1 = (f32[1024,1024]{1,0:T(8,128)S(1)}, bf16[1024,256]{1,0:T(8,128)(2,1)S(1)}, bf16[4,64,1024]{2,1,0:T(8,128)(2,1)S(1)}) custom-call(bf16[1024,1024]{1,0:T(8,128)(2,1)} %bitcast.6, bf16[32,1024]{1,0:T(8,128)(2,1)} %bitcast.7, s32[2,1024]{1,0:T(2,128)} %bitcast.8, s32[1,1024]{1,0:T(1,128)} %keep_hbm.1, bf16[4,1024,2816]{2,1,0:T(8,128)(2,1)} %win_hbm.1, ...), custom_call_target="tpu_custom_call" | custom-call | tf_op jit(solution)/shard_map/moe_layer/pallas_call | solution.py:356
  95.0 1.6 %moe_finish.1 = bf16[1024,1024]{1,0:T(8,128)(2,1)} custom-call(f32[1024,1024]{1,0:T(8,128)S(1)} %get-tuple-element.8.acc, bf16[1024,256]{1,0:T(8,128)(2,1)S(1)} %get-tuple-element.9.cw, bf16[4,64,1024]{2,1,0:T(8,128)(2,1)S(1)} %get-tuple-element.10.y), custom_call_target="tpu_custom_call" | custom-call | tf_op jit(solution)/shard_map/moe_finish/pallas_call | solution.py:386

commit v10 on v9

--- a/solution.py
+++ b/solution.py
@@ -49,8 +49,8 @@
         pltpu.make_async_copy(ids_hbm, ids, in_sem.at[0]),
         pltpu.make_async_copy(keep_hbm, keep, in_sem.at[1]),
     ] + [
-        pltpu.make_async_copy(tok_hbm.at[:, part], tok.at[:, part], in_sem.at[2 + i]) for i, part in enumerate(parts)
-    ] + [pltpu.make_async_copy(wg_hbm, wg, in_sem.at[4])]
+        pltpu.make_async_copy(tok_hbm.at[:, part], tok.at[:, part], wi_sem.at[i]) for i, part in enumerate(parts)
+    ] + [pltpu.make_async_copy(wg_hbm, wg, in_sem.at[2])]
     for copy in small:
         copy.start()
 
@@ -115,15 +115,15 @@
 
     def y_send(i, p):
         at = pl.ds(*Y_PIECES[i])
-        return copy_to(p, ys.at[p, at], yr.at[p, at], ys_sem.at[0], yr_sem.at[(0, 1, 2 + p // 2)[i]])
+        return copy_to(p, ys.at[p, at], yr.at[p, at], ys_sem.at[0], yr_sem.at[i])
 
     def y_wait(i, first, count):
         at, places = pl.ds(*Y_PIECES[i]), pl.ds(first, count)
-        copy_to(1, ys.at[places, at], yr.at[places, at], ys_sem.at[0], yr_sem.at[(0, 1, 2 + first // 2)[i]]).wait_recv()
+        copy_to(1, ys.at[places, at], yr.at[places, at], ys_sem.at[0], yr_sem.at[i]).wait_recv()
 
     def end_send(p, first, count):
         at = pl.ds(first, count)
-        return copy_to(p, ys.at[p, experts_here - 1, at], y_end.at[p - 4, at], ys_sem.at[0], yr_sem.at[4])
+        return copy_to(p, ys.at[p, experts_here - 1, at], y_end.at[p - 4, at], ys_sem.at[0], yr_sem.at[3])
 
     def first_slot(e, p):
         return peer_of(me, ORDER[p]) * (experts_here * cap) + e * cap
@@ -319,9 +319,8 @@
 
     y_wait(1, 4, 4)
     add_rows(rows, lambda at: yr[4:8, 2, :, at])
-    y_wait(2, 1, 1)
+    y_wait(2, 1, 3)
     add_rows(0, lambda at: yr[0:2, 2:4, :, at])
-    y_wait(2, 2, 2)
     add_rows(4 * cap, lambda at: yr[2:4, 2:4, :, at])
     cw_end[...] = cw[1, :, 2 * rows - 4 * cap:]
     @pl.when(me == 7)
@@ -330,7 +329,7 @@
 
     sent = pl.ds(1, groups - 1)
     copy_to(1, xs.at[sent], xr.at[sent], xs_sem.at[0], xr_sem.at[0]).wait_send()
-    copy_to(1, ys.at[4:8, 0], y_end, ys_sem.at[0], yr_sem.at[4]).wait_recv()
+    copy_to(1, ys.at[4:8, 0], y_end, ys_sem.at[0], yr_sem.at[3]).wait_recv()
     copy_to(1, ys.at[sent], yr.at[sent], ys_sem.at[0], yr_sem.at[0]).wait_send()
 
 
@@ -377,8 +376,8 @@
                 vmem((2, dim, hidden), bf16),
                 vmem((2, hidden, dim), bf16),
                 vmem((here // 2, token_count, 2 * rows), bf16),
-                dma((5,)), dma((2,)), dma((2,)),
-                dma((1,)), dma((3,)), dma((1,)), dma((5,)), dma((2,)),
+                dma((3,)), dma((2,)), dma((2,)),
+                dma((1,)), dma((3,)), dma((1,)), dma((4,)), dma((2,)),
             ],
             compiler_params=pltpu.CompilerParams(collective_id=0, has_side_effects=True, vmem_limit_bytes=56 * 2**20),
             name="moe_layer",

time: 96.7 us -> 96.7 us (level)
  no operation moved by 1% of the time
where the time goes in v10:
time: 96.7 us; the launch traced here: 96.5 us
  Pallas kernels  96.5 us (100%)
    pallas_call x1, Pallas kernels, local_layer(): pl.pallas_call(functools.partial(layer_kernel, cap), out_shape=(vmem((tok...  95 us

profile of v10, /device:TPU:0, one launch (start us, length us, event | category | flops | bytes accessed | tf_op | source)
XLA Modules:
  0.0 96.5 jit_solution(1243336962733059258)
XLA Ops:
  0.0 95.0 %moe_layer.1 = (f32[1024,1024]{1,0:T(8,128)S(1)}, bf16[1024,256]{1,0:T(8,128)(2,1)S(1)}, bf16[4,64,1024]{2,1,0:T(8,128)(2,1)S(1)}) custom-call(bf16[1024,1024]{1,0:T(8,128)(2,1)} %bitcast.6, bf16[32,1024]{1,0:T(8,128)(2,1)} %bitcast.7, s32[2,1024]{1,0:T(2,128)} %bitcast.8, s32[1,1024]{1,0:T(1,128)} %keep_hbm.1, bf16[4,1024,2816]{2,1,0:T(8,128)(2,1)} %win_hbm.1, ...), custom_call_target="tpu_custom_call" | custom-call | tf_op jit(solution)/shard_map/moe_layer/pallas_call | solution.py:355
  95.0 1.6 %moe_finish.1 = bf16[1024,1024]{1,0:T(8,128)(2,1)} custom-call(f32[1024,1024]{1,0:T(8,128)S(1)} %get-tuple-element.8.acc, bf16[1024,256]{1,0:T(8,128)(2,1)S(1)} %get-tuple-element.9.cw, bf16[4,64,1024]{2,1,0:T(8,128)(2,1)S(1)} %get-tuple-element.10.y), custom_call_target="tpu_custom_call" | custom-call | tf_op jit(solution)/shard_map/moe_finish/pallas_call | solution.py:385

commit v11 on v10

--- a/solution.py
+++ b/solution.py
@@ -9,7 +9,7 @@
 
 MESH = pl.DeviceIdType.MESH
 ORDER = (0, 1, 6, 7, 2, 4, 3, 5)
-SENDS = (2, 3, 4, 5, 6, 7, 1)
+SENDS = (2, 4, 5, 3, 6, 7, 1)
 X_PIECES = ((0, 1), (1, 1), (2, 2))
 Y_PIECES = ((0, 2), (2, 1), (2, 2))
 NEAR, FAR = (4, 5, 6, 7), (2, 3, 1)
@@ -32,10 +32,11 @@
 
 def layer_kernel(
     cap, tok_hbm, wg_hbm, ids_hbm, keep_hbm, win_hbm, wout_hbm, acc, cw_end, y_end,
-    tok, wg, ids, keep, slot_of, gates, cols, slots, hop, dmat, xs, xr, ys, yr, hid, wi, wo, cw,
-    in_sem, wi_sem, wo_sem, xs_sem, xr_sem, ys_sem, yr_sem, hop_sem,
+    tok, wg, ids, keep, slot_of, gates, cols, slots, hop, dmat, out_rows, xr, yr, hid, wi, wo, cw,
+    in_sem, wi_sem, wo_sem, sent_sem, xr_sem, yr_sem, hop_sem,
 ):
     me = lax.axis_index("ep")
+    xs, ys = out_rows.at[0], out_rows.at[1]
     experts_here = win_hbm.shape[0]
     tokens, dim = tok.shape
     experts = wg.shape[0]
@@ -97,33 +98,33 @@
 
     def x_send(i, p):
         at = pl.ds(*X_PIECES[i])
-        return copy_to(p, xs.at[p, at], xr.at[p, at], xs_sem.at[0], xr_sem.at[i])
+        return copy_to(p, xs.at[p, at], xr.at[p, at], sent_sem.at[0], xr_sem.at[i])
 
     def far_send(e, first, count):
         at = pl.ds(first, count)
-        return copy_to(2, xs.at[2, e, at], xr.at[2, e, at], xs_sem.at[0], xr_sem.at[2])
+        return copy_to(2, xs.at[2, e, at], xr.at[2, e, at], sent_sem.at[0], xr_sem.at[2])
 
     def hop_send(e):
-        return copy_to(5, xs.at[2, e, pl.ds(cap - HOP, HOP)], hop, xs_sem.at[0], hop_sem.at[0])
+        return copy_to(5, xs.at[2, e, pl.ds(cap - HOP, HOP)], hop, sent_sem.at[0], hop_sem.at[0])
 
     def hop_on(e):
         return copy_to(4, hop, xr.at[2, e, pl.ds(cap - HOP, HOP)], hop_sem.at[1], xr_sem.at[2])
 
     def x_wait(i):
         at, places = pl.ds(*X_PIECES[i]), pl.ds(1, groups - 1)
-        copy_to(1, xs.at[places, at], xr.at[places, at], xs_sem.at[0], xr_sem.at[i]).wait_recv()
+        copy_to(1, xs.at[places, at], xr.at[places, at], sent_sem.at[0], xr_sem.at[i]).wait_recv()
 
     def y_send(i, p):
         at = pl.ds(*Y_PIECES[i])
-        return copy_to(p, ys.at[p, at], yr.at[p, at], ys_sem.at[0], yr_sem.at[i])
+        return copy_to(p, ys.at[p, at], yr.at[p, at], sent_sem.at[0], yr_sem.at[i])
 
     def y_wait(i, first, count):
         at, places = pl.ds(*Y_PIECES[i]), pl.ds(first, count)
-        copy_to(1, ys.at[places, at], yr.at[places, at], ys_sem.at[0], yr_sem.at[i]).wait_recv()
+        copy_to(1, ys.at[places, at], yr.at[places, at], sent_sem.at[0], yr_sem.at[i]).wait_recv()
 
     def end_send(p, first, count):
         at = pl.ds(first, count)
-        return copy_to(p, ys.at[p, experts_here - 1, at], y_end.at[p - 4, at], ys_sem.at[0], yr_sem.at[3])
+        return copy_to(p, ys.at[p, experts_here - 1, at], y_end.at[p - 4, at], sent_sem.at[0], yr_sem.at[3])
 
     def first_slot(e, p):
         return peer_of(me, ORDER[p]) * (experts_here * cap) + e * cap
@@ -328,9 +329,9 @@
         hop_on(3).wait_send()
 
     sent = pl.ds(1, groups - 1)
-    copy_to(1, xs.at[sent], xr.at[sent], xs_sem.at[0], xr_sem.at[0]).wait_send()
-    copy_to(1, ys.at[4:8, 0], y_end, ys_sem.at[0], yr_sem.at[3]).wait_recv()
-    copy_to(1, ys.at[sent], yr.at[sent], ys_sem.at[0], yr_sem.at[0]).wait_send()
+    copy_to(1, ys.at[4:8, 0], y_end, sent_sem.at[0], yr_sem.at[3]).wait_recv()
+    everything = out_rows.at[:, sent]
+    copy_to(1, everything, everything, sent_sem.at[0], xr_sem.at[0]).wait_send()
 
 
 def finish_kernel(acc, cw, y, out, buf, sem):
@@ -368,8 +369,7 @@
                 vmem((2, 8, 2 * rows), f32),
                 vmem((HOP, dim), bf16),
                 vmem((rows, token_count), bf16),
-                vmem((groups, here, cap, dim), bf16),
-                vmem((groups, here, cap, dim), bf16),
+                vmem((2, groups, here, cap, dim), bf16),
                 vmem((groups, here, cap, dim), bf16),
                 vmem((groups, here, cap, dim), bf16),
                 vmem((rows, hidden), bf16),
@@ -377,7 +377,7 @@
                 vmem((2, hidden, dim), bf16),
                 vmem((here // 2, token_count, 2 * rows), bf16),
                 dma((3,)), dma((2,)), dma((2,)),
-                dma((1,)), dma((3,)), dma((1,)), dma((4,)), dma((2,)),
+                dma((1,)), dma((3,)), dma((4,)), dma((2,)),
             ],
             compiler_params=pltpu.CompilerParams(collective_id=0, has_side_effects=True, vmem_limit_bytes=56 * 2**20),
             name="moe_layer",

time: 96.7 us -> 96.7 us (level)
  no operation moved by 1% of the time
where the time goes in v11:
time: 96.7 us; the launch traced here: 96.5 us
  Pallas kernels  96.5 us (100%)
    pallas_call x1, Pallas kernels, local_layer(): pl.pallas_call(functools.partial(layer_kernel, cap), out_shape=(vmem((tok...  95 us

profile of v11, /device:TPU:0, one launch (start us, length us, event | category | flops | bytes accessed | tf_op | source)
XLA Modules:
  0.0 96.5 jit_solution(15326467558320795750)
XLA Ops:
  0.0 95.0 %moe_layer.1 = (f32[1024,1024]{1,0:T(8,128)S(1)}, bf16[1024,256]{1,0:T(8,128)(2,1)S(1)}, bf16[4,64,1024]{2,1,0:T(8,128)(2,1)S(1)}) custom-call(bf16[1024,1024]{1,0:T(8,128)(2,1)} %bitcast.6, bf16[32,1024]{1,0:T(8,128)(2,1)} %bitcast.7, s32[2,1024]{1,0:T(2,128)} %bitcast.8, s32[1,1024]{1,0:T(1,128)} %keep_hbm.1, bf16[4,1024,2816]{2,1,0:T(8,128)(2,1)} %win_hbm.1, ...), custom_call_target="tpu_custom_call" | custom-call | tf_op jit(solution)/shard_map/moe_layer/pallas_call | solution.py:356
  95.0 1.6 %moe_finish.1 = bf16[1024,1024]{1,0:T(8,128)(2,1)} custom-call(f32[1024,1024]{1,0:T(8,128)S(1)} %get-tuple-element.8.acc, bf16[1024,256]{1,0:T(8,128)(2,1)S(1)} %get-tuple-element.9.cw, bf16[4,64,1024]{2,1,0:T(8,128)(2,1)S(1)} %get-tuple-element.10.y), custom_call_target="tpu_custom_call" | custom-call | tf_op jit(solution)/shard_map/moe_finish/pallas_call | solution.py:385

commit v12 on v11

--- a/solution.py
+++ b/solution.py
@@ -171,14 +171,14 @@
 
         @pl.when(e == 3)
         def _():
-            @pl.when(me == 3)
+            @pl.when((me == 3) | (me == 1))
             def _():
                 hop_send(3).start()
                 far_send(2, 0, cap).start()
                 if HOP < cap:
                     far_send(3, 0, cap - HOP).start()
 
-            @pl.when(me != 3)
+            @pl.when((me != 3) & (me != 1))
             def _():
                 x_send(2, 2).start()
 
@@ -241,7 +241,7 @@
 
         wi_copy(e).wait()
 
-        @pl.when((e == 1) & (me == 7))
+        @pl.when((e == 1) & ((me == 7) | (me == 5)))
         def _():
             hop_send(3).wait_recv()
             hop_on(3).start()
@@ -324,7 +324,7 @@
     add_rows(0, lambda at: yr[0:2, 2:4, :, at])
     add_rows(4 * cap, lambda at: yr[2:4, 2:4, :, at])
     cw_end[...] = cw[1, :, 2 * rows - 4 * cap:]
-    @pl.when(me == 7)
+    @pl.when((me == 7) | (me == 5))
     def _():
         hop_on(3).wait_send()
 

time: 96.7 us -> 96.7 us (level)
  no operation moved by 1% of the time
where the time goes in v12:
time: 96.7 us; the launch traced here: 96.2 us
  Pallas kernels  96.1 us (99%)
    pallas_call x1, Pallas kernels, local_layer(): pl.pallas_call(functools.partial(layer_kernel, cap), out_shape=(vmem((tok...  94.6 us

profile of v12, /device:TPU:0, one launch (start us, length us, event | category | flops | bytes accessed | tf_op | source)
XLA Modules:
  0.0 96.2 jit_solution(7342797370402313688)
XLA Ops:
  0.0 94.6 %moe_layer.1 = (f32[1024,1024]{1,0:T(8,128)S(1)}, bf16[1024,256]{1,0:T(8,128)(2,1)S(1)}, bf16[4,64,1024]{2,1,0:T(8,128)(2,1)S(1)}) custom-call(bf16[1024,1024]{1,0:T(8,128)(2,1)} %bitcast.6, bf16[32,1024]{1,0:T(8,128)(2,1)} %bitcast.7, s32[2,1024]{1,0:T(2,128)} %bitcast.8, s32[1,1024]{1,0:T(1,128)} %keep_hbm.1, bf16[4,1024,2816]{2,1,0:T(8,128)(2,1)} %win_hbm.1, ...), custom_call_target="tpu_custom_call" | custom-call | tf_op jit(solution)/shard_map/moe_layer/pallas_call | solution.py:356
  94.6 1.6 %moe_finish.1 = bf16[1024,1024]{1,0:T(8,128)(2,1)} custom-call(f32[1024,1024]{1,0:T(8,128)S(1)} %get-tuple-element.8.acc, bf16[1024,256]{1,0:T(8,128)(2,1)S(1)} %get-tuple-element.9.cw, bf16[4,64,1024]{2,1,0:T(8,128)(2,1)S(1)} %get-tuple-element.10.y), custom_call_target="tpu_custom_call" | custom-call | tf_op jit(solution)/shard_map/moe_finish/pallas_call | solution.py:385
